TPU v7x, 128 devices: a whole 4x4x4 slice. The times are simulated.
128 devices in a mesh: gx: 4 (over x), gy: 4 (over y), gz: 8 (over z, core).
Axes of the slice: x: 4, y: 4, z: 4, core: 2. Of those that a mesh axis runs over, the one named last changes fastest.
Arguments:
- fields: bfloat16 [16384, 2048], P(('gx', 'gy', 'gz')), may hold values from -6 to 6
- coordinates: float32 [3, 2097152], P(None, ('gx', 'gy', 'gz')), may hold values from -1 to 1
- element_rank: int32 [2097152, 1], P(('gx', 'gy', 'gz')), may hold values from 0 to 127; in each aligned block of 16384 rows (0 to 16383, 16384 to 32767, ...) at most 160 rows name the same one
- element_slot: int32 [2097152], P(('gx', 'gy', 'gz')), may hold values from 0 to 127
Outputs:
- samples: float32 [4, 2097152], P(None, ('gx', 'gy', 'gz'))
Inputs may be any that keep to these rules, and one draw needn't show every extreme that they name: `element_rank`: among the probes of one device no rank is named by more than 160 probes, and in some devices' blocks one rank is named by exactly 160.
All inputs are finite; a program needn't handle non-finite values.
Results may differ from a plain program's by a relative error of at most 0.0024.
Values sent between devices are 32-bit elements; how exact they have to be, the bound alone decides.
A program may use at most 64 MiB of HBM per device.

v0:
```python
import functools

import jax
import jax.numpy as jnp
import numpy as np
from jax import lax
from jax.experimental import pallas as pl
from jax.experimental.pallas import tpu as pltpu
from jax.sharding import PartitionSpec as P

AXES = ("gx", "gy", "gz")
F32, BF16 = jnp.float32, jnp.bfloat16
LANES = 128
CHUNK = 256
GROUP = 4

gll_points = np.array(
    [
        -1.0,
        -0.8717401485096066,
        -0.5917001814331423,
        -0.2092992179024789,
        0.2092992179024789,
        0.5917001814331423,
        0.8717401485096066,
        1.0,
    ]
)
gll_scale = np.array(
    [1.0 / np.prod([gll_points[a] - gll_points[b] for b in range(8) if b != a]) for a in range(8)]
)
node_table = np.stack(
    [gll_scale] + [np.roll(gll_points, -k) for k in range(1, 8)], axis=0
).reshape(64, 1)


def iota_bf16(shape):
    return lax.broadcasted_iota(jnp.int32, shape, 0).astype(F32).astype(BF16)


def spread(row, count):
    return jnp.broadcast_to(row, (count, row.shape[1])).astype(BF16)


def route(count, blocks, rank_ref, coords_ref, slot_ref, prefix_ref, send_ref, row_ref, lane_ref, acc_ref):
    probes = rank_ref.shape[1]
    group = max(1, CHUNK // count)
    targets = lax.broadcasted_iota(jnp.int32, (count, CHUNK), 0)

    def place(step, carry):
        masks, hots, ranks = [], [], []
        for g in range(group):
            at = pl.ds(pl.multiple_of((step * group + g) * CHUNK, CHUNK), CHUNK)
            rank = rank_ref[:, at]
            mask = targets == jnp.broadcast_to(rank, (count, CHUNK))
            masks.append(mask)
            hots.append(jnp.where(mask, 1.0, 0.0).astype(BF16))
            ranks.append(rank.astype(F32))
        counted = jnp.dot(jnp.concatenate(hots, axis=0), prefix_ref[...], preferred_element_type=F32)
        for g in range(group):
            at = pl.ds(pl.multiple_of((step * group + g) * CHUNK, CHUNK), CHUNK)
            piece = counted[g * count : (g + 1) * count]
            place_in = jnp.where(masks[g], piece[:, :CHUNK] + carry, 0.0)
            position = jnp.sum(place_in, axis=0, keepdims=True) - 1.0
            block = jnp.floor(position * (1.0 / LANES))
            lane_ref[:, at] = position - block * LANES
            row_ref[:, at] = block * count + ranks[g]
            carry = carry + piece[:, CHUNK:]
        return carry

    lax.fori_loop(0, probes // (CHUNK * group), place, jnp.zeros((count, CHUNK), F32))

    rows = count * blocks
    part_lanes = LANES // 2
    row_ids = iota_bf16((rows, CHUNK))
    lane_ids = iota_bf16((part_lanes, CHUNK))
    one, zero = jnp.ones((), BF16), jnp.zeros((), BF16)
    acc_ref[...] = jnp.zeros_like(acc_ref)

    def scatter(step, _):
        row_hots, lane_parts = [], []
        for g in range(4):
            at = pl.ds(pl.multiple_of((step * 4 + g) * CHUNK, CHUNK), CHUNK)
            row, lane = row_ref[:, at], lane_ref[:, at]
            upper = lane >= float(part_lanes)
            halves = [jnp.where(upper, -1.0, row), jnp.where(upper, row, -1.0)]
            row_hots.append(
                jnp.concatenate([jnp.where(row_ids == spread(part, rows), one, zero) for part in halves], axis=0)
            )
            here = lane_ids == spread(jnp.where(upper, lane - float(part_lanes), lane), part_lanes)
            parts = []
            for v in range(3):
                value = coords_ref[v : v + 1, at]
                high = value.astype(BF16).astype(F32)
                parts += [high, value - high]
            parts.append(slot_ref[:, at].astype(F32))
            chosen = [jnp.where(here, spread(part, part_lanes), zero) for part in parts]
            chosen.append(jnp.zeros((part_lanes, CHUNK), BF16))
            lane_parts.append(jnp.concatenate(chosen, axis=0))
        acc_ref[...] += lax.dot_general(
            jnp.concatenate(row_hots, axis=1),
            jnp.concatenate(lane_parts, axis=1),
            (((1,), (1,)), ((), ())),
            preferred_element_type=F32,
        )
        return 0

    lax.fori_loop(0, probes // (4 * CHUNK), scatter, 0)
    left = lax.broadcasted_iota(jnp.int32, (count, LANES), 1) < part_lanes
    for b in range(blocks):
        for v in range(4):
            sides = []
            for h in range(2):
                first = h * rows + b * count
                both = acc_ref[first : first + count, v * LANES : (v + 1) * LANES]
                sides.append(both + pltpu.roll(both, part_lanes, 1))
            send_ref[v * blocks + b] = jnp.where(left, sides[0], sides[1])


def lagrange(coord, nodes_ref):
    weight = nodes_ref[0:8, :]
    spread_coord = jnp.broadcast_to(coord, (8, LANES))
    for k in range(1, 8):
        weight = weight * (spread_coord - nodes_ref[8 * k : 8 * k + 8, :])
    return weight


def interpolate(blocks, block, sources, recv_ref, fields_ref, nodes_ref, values_ref, picker_ref):
    depth = fields_ref.shape[1]
    elements = depth // 8
    zero = jnp.zeros((), BF16)
    ids = iota_bf16((16, LANES))
    weights = []
    for j, source in enumerate(sources):
        r, s, t, slot = [recv_ref[v * blocks + block, pl.ds(source, 1), :] for v in range(4)]
        weights.append((lagrange(r, nodes_ref), lagrange(s, nodes_ref)))
        weight_t = lagrange(t, nodes_ref)
        columns = slice(j * LANES, (j + 1) * LANES)
        masks = [ids == spread(slot - float(16 * k), 16) for k in range(elements // 16)]
        for c in range(8):
            weight = spread(weight_t[c : c + 1, :], 16)
            for k in range(elements // 16):
                at = c * elements + k * 16
                picker_ref[at : at + 16, columns] = jnp.where(masks[k], weight, zero)
    along = jnp.dot(fields_ref[...], picker_ref[...], preferred_element_type=F32)
    for j, source in enumerate(sources):
        weight_r, weight_s = weights[j]
        columns = slice(j * LANES, (j + 1) * LANES)
        factors = [jnp.broadcast_to(weight_r[a : a + 1, :], (8, LANES)) for a in range(8)]
        for f in range(4):
            total = along[f * 64 : f * 64 + 8, columns] * factors[0]
            for a in range(1, 8):
                total += along[f * 64 + a * 8 : f * 64 + a * 8 + 8, columns] * factors[a]
            values_ref[f * blocks + block, pl.ds(source, 1), :] = jnp.sum(
                total * weight_s, axis=0, keepdims=True
            )


def sample_kernel(
    sizes,
    blocks,
    rank_ref,
    coords_ref,
    slot_ref,
    prefix_ref,
    fields_ref,
    nodes_ref,
    back_ref,
    row_ref,
    lane_ref,
    acc_ref,
    send_ref,
    recv_ref,
    values_ref,
    picker_even,
    picker_odd,
    out_sem,
    in_sem,
    back_out_sem,
    back_in_sem,
    own_sem,
):
    count = sizes[0] * sizes[1] * sizes[2]
    me = (lax.axis_index("gx") * sizes[1] + lax.axis_index("gy")) * sizes[2] + lax.axis_index("gz")
    mesh_ids = pl.DeviceIdType.MESH

    def coordinates_of(device):
        return (device // (sizes[1] * sizes[2]), (device // sizes[2]) % sizes[1], device % sizes[2])

    def each(first, last, act):
        def body(step, _):
            act(step)
            return 0

        lax.fori_loop(first, last, body, 0)

    def behind(step):
        return lax.rem(me + count - step, count)

    def outward(step):
        other = lax.rem(me + step, count)
        return pltpu.make_async_remote_copy(
            src_ref=send_ref.at[:, other],
            dst_ref=recv_ref.at[:, me],
            send_sem=out_sem.at[step],
            recv_sem=in_sem.at[step],
            device_id=coordinates_of(other),
            device_id_type=mesh_ids,
        )

    def backward(step):
        other = behind(step)
        return pltpu.make_async_remote_copy(
            src_ref=values_ref.at[:, other],
            dst_ref=back_ref.at[:, me],
            send_sem=back_out_sem.at[step],
            recv_sem=back_in_sem.at[step],
            device_id=coordinates_of(other),
            device_id_type=mesh_ids,
        )

    barrier = pltpu.get_barrier_semaphore()
    each(
        1,
        count,
        lambda step: pl.semaphore_signal(
            barrier, inc=1, device_id=coordinates_of(lax.rem(me + step, count)), device_id_type=mesh_ids
        ),
    )
    route(count, blocks, rank_ref, coords_ref, slot_ref, prefix_ref, send_ref, row_ref, lane_ref, acc_ref)
    pl.semaphore_wait(barrier, count - 1)
    each(1, count, lambda step: outward(step).start())
    own = pltpu.make_async_copy(send_ref.at[:, me], recv_ref.at[:, me], own_sem.at[0])
    own.start()
    own.wait()
    own_back = pltpu.make_async_copy(values_ref.at[:, me], back_ref.at[:, me], own_sem.at[1])
    pickers = [picker_even, picker_odd]

    def reply(group):
        for j in range(GROUP):
            step = group * GROUP + j
            if j == 0:

                @pl.when(step == 0)
                def _():
                    own_back.start()

                @pl.when(step > 0)
                def _():
                    backward(step).start()

            else:
                backward(step).start()

    def body(group, _):
        sources = []
        for j in range(GROUP):
            step = group * GROUP + j
            if j == 0:

                @pl.when(step > 0)
                def _():
                    outward(step).wait_recv()

            else:
                outward(step).wait_recv()
            sources.append(behind(step))
        for block in range(blocks):
            interpolate(blocks, block, sources, recv_ref, fields_ref, nodes_ref, values_ref, pickers[block % 2])

        @pl.when(group > 0)
        def _():
            reply(group - 1)

        return 0

    groups = count // GROUP
    lax.fori_loop(0, groups, body, 0)
    each(1, count, lambda step: outward(step).wait_send())
    reply(groups - 1)
    each(1, count, lambda step: backward(step).wait())
    own_back.wait()


def return_kernel(blocks, values_ref, row_ref, lane_ref, out_ref, table_ref):
    probes = row_ref.shape[1]
    count = values_ref.shape[1]
    rows = blocks * count
    for f in range(4):
        table = jnp.concatenate([values_ref[f * blocks + b] for b in range(blocks)], axis=0)
        table_ref[f * LANES : (f + 1) * LANES, :] = table.T.astype(BF16)
    row_ids = iota_bf16((rows, CHUNK))
    lane_ids = lax.broadcasted_iota(jnp.int32, (LANES, CHUNK), 0).astype(F32)

    def body(step, _):
        for g in range(4):
            at = pl.ds(pl.multiple_of((step * 4 + g) * CHUNK, CHUNK), CHUNK)
            hot = jnp.where(row_ids == spread(row_ref[:, at], rows), jnp.ones((), BF16), jnp.zeros((), BF16))
            picked = jnp.dot(table_ref[...], hot, preferred_element_type=F32)
            here = lane_ids == jnp.broadcast_to(lane_ref[:, at], (LANES, CHUNK))
            for f in range(4):
                out_ref[f : f + 1, at] = jnp.sum(
                    jnp.where(here, picked[f * LANES : (f + 1) * LANES], 0.0), axis=0, keepdims=True
                )
        return 0

    lax.fori_loop(0, probes // (4 * CHUNK), body, 0)


VMEM = pl.BlockSpec(memory_space=pltpu.VMEM)


def call(kernel, inputs, outputs, scratch, **options):
    return pl.pallas_call(
        kernel,
        out_shape=outputs,
        in_specs=[VMEM] * inputs,
        out_specs=jax.tree.map(lambda _: VMEM, outputs),
        scratch_shapes=scratch,
        compiler_params=pltpu.CompilerParams(vmem_limit_bytes=48 << 20, **options),
    )


def local(sizes, fields, coordinates, element_rank, element_slot):
    count = sizes[0] * sizes[1] * sizes[2]
    probes = element_slot.shape[0]
    elements = fields.shape[0]
    capacity = 5 * probes // (4 * count)
    blocks = -(-capacity // LANES)
    layout = jax.ShapeDtypeStruct((4 * blocks, count, LANES), F32)
    line = jax.ShapeDtypeStruct((1, probes), F32)

    lower = np.arange(CHUNK)
    prefix = np.concatenate([lower[:, None] <= lower[None, :], np.ones((CHUNK, CHUNK))], axis=1)
    turned = fields.reshape(elements, 256, 8).transpose(1, 2, 0).reshape(256, 8 * elements)
    nodes = jnp.broadcast_to(jnp.asarray(node_table, F32), (64, LANES))
    picker = pltpu.VMEM((8 * elements, GROUP * LANES), BF16)
    buffer = pltpu.VMEM(layout.shape, F32)
    arrivals = pltpu.SemaphoreType.DMA((count,))
    returned, row, lane = call(
        functools.partial(sample_kernel, sizes, blocks),
        6,
        (layout, line, line),
        [pltpu.VMEM((2 * count * blocks, 4 * LANES), F32)]
        + [buffer] * 3
        + [picker] * 2
        + [arrivals] * 4
        + [pltpu.SemaphoreType.DMA((2,))],
        collective_id=0,
        has_side_effects=True,
    )(
        element_rank.reshape(1, probes),
        coordinates,
        element_slot.reshape(1, probes),
        jnp.asarray(prefix, BF16),
        turned,
        nodes,
    )
    return call(
        functools.partial(return_kernel, blocks),
        3,
        jax.ShapeDtypeStruct((4, probes), F32),
        [pltpu.VMEM((4 * LANES, count * blocks), BF16)],
    )(returned, row, lane)


def solution(mesh):
    sizes = tuple(mesh.shape[axis] for axis in AXES)
    placed = (P(AXES, None), P(None, AXES), P(AXES, None), P(AXES))
    return jax.shard_map(
        functools.partial(local, sizes),
        mesh=mesh,
        in_specs=placed,
        out_specs=P(None, AXES),
        check_vma=False,
    )
```

profile of v0, /device:TPU:1, one launch (start us, length us, event | category | flops | bytes accessed | tf_op | source)
XLA Modules:
  0.0 83.8 jit_solution(13401056221246610955)
XLA Ops:
  0.0 1.3 %copy.8 = bf16[128,2048]{0,1:T(8,128)(2,1)S(1)} copy(bf16[128,2048]{1,0:T(8,128)(2,1)} %param.6) | data formatting | bytes 1048576 | tf_op args[0]
  1.3 0.0 copy-start
  1.3 0.0 copy-start.1
  1.3 0.0 copy-start.2
  1.4 0.0 copy-start.3
  1.4 0.1 copy.11
  1.5 0.0 copy-start.4
  1.5 0.7 copy-done.4
  2.2 0.1 broadcast_in_dim.8.nodes_ref
  2.2 0.0 copy-done
  2.3 0.1 copy-done.1
  2.4 0.0 copy-done.2
  2.4 0.0 copy-done.3
  2.4 73.3 %shard_map.64 = (f32[8,128,128]{2,1,0:T(8,128)S(1)}, f32[1,16384]{1,0:T(1,128)S(1)}, f32[1,16384]{1,0:T(1,128)S(1)}) custom-call(s32[1,16384]{1,0:T(1,128)S(1)} %bitcast.10, f32[3,16384]{1,0:T(4,128)S(1)} %copy-done, s32[1,16384]{1,0:T(1,128)S(1)} %bitcast.11, bf16[256,512]{1,0:T(8,128)(2,1)S(1)} %copy-done.1, bf16[256,1024]{1,0:T(8,128)(2,1)S(1)} %bitcast.9, ...), custom_call_target="tpu_custom_call" | custom-call | tf_op jit(solution)/shard_map/pallas_call | solution.py:340
  75.7 8.1 %shard_map.65 = f32[4,16384]{1,0:T(4,128)} custom-call(f32[8,128,128]{2,1,0:T(8,128)S(1)} %get-tuple-element.8.values_ref, f32[1,16384]{1,0:T(1,128)S(1)} %get-tuple-element.9.row_ref, f32[1,16384]{1,0:T(1,128)S(1)} %get-tuple-element.10.lane_ref), custom_call_target="tpu_custom_call" | custom-call | tf_op jit(solution)/shard_map/pallas_call | solution.py:359
Async XLA Ops:
  1.3 1.0 %copy-start = (f32[3,16384]{1,0:T(4,128)S(1)}, f32[3,16384]{1,0:T(4,128)}, u32[]{:S(2)}) copy-start(f32[3,16384]{1,0:T(4,128)} %coords_ref.1) | copy-start | bytes 589828
  1.3 1.0 %copy-start.1 = (bf16[256,512]{1,0:T(8,128)(2,1)S(1)}, bf16[256,512]{1,0:T(8,128)(2,1)}, u32[]{:S(2)}) copy-start(bf16[256,512]{1,0:T(8,128)(2,1)} %constant.5.clone.prefix_ref) | copy-start | bytes 786436
  1.3 1.0 %copy-start.2 = (s32[16384,1]{0,1:T(1,128)S(1)}, s32[16384,1]{0,1:T(1,128)}, u32[]{:S(2)}) copy-start(s32[16384,1]{0,1:T(1,128)} %param.8) | copy-start | bytes 196612
  1.4 1.0 %copy-start.3 = (s32[16384]{0:T(1024)S(1)}, s32[16384]{0:T(1024)}, u32[]{:S(2)}) copy-start(s32[16384]{0:T(1024)} %param.9) | copy-start | bytes 196612
  1.5 0.7 copy-start.4
where the time goes:
time: 84 us; the launch traced here: 83.8 us
  Pallas kernels  81.4 us (97%)
  local copies, waits for them, and re-layouts  2.3 us (3%)
    pallas_call x1, Pallas kernels, local(): call(functools.partial(sample_kernel, sizes, blocks), 6, (layout, line, l...  73.3 us
    pallas_call x1, Pallas kernels, local(): call(functools.partial(return_kernel, blocks), 3, jax.ShapeDtypeStruct((4...  8.11 us
    unnamed x12, local copies, waits for them, and re-layouts  2.23 us

commit v1 on v0

v1 whole, which is shorter than its diff:
```python
import functools

import jax
import jax.numpy as jnp
import numpy as np
from jax import lax
from jax.experimental import pallas as pl
from jax.experimental.pallas import tpu as pltpu
from jax.sharding import PartitionSpec as P

AXES = ("gx", "gy", "gz")
F32, BF16 = jnp.float32, jnp.bfloat16
LANES = 128
CHUNK = 256
PIECE = 32
BLOCKS = 5
PLACED = 8
GATHERED = 4

gll_points = np.array(
    [
        -1.0,
        -0.8717401485096066,
        -0.5917001814331423,
        -0.2092992179024789,
        0.2092992179024789,
        0.5917001814331423,
        0.8717401485096066,
        1.0,
    ]
)
gll_scale = np.array(
    [1.0 / np.prod([gll_points[a] - gll_points[b] for b in range(8) if b != a]) for a in range(8)]
)
node_table = np.stack(
    [gll_scale] + [np.roll(gll_points, -k) for k in range(1, 8)], axis=0
).reshape(64, 1)

RING = [0, 1, 2, 1]


def far_to_near(sizes):
    def hops(q):
        x, y, z = q // (sizes[1] * sizes[2]), (q // sizes[2]) % sizes[1], q % sizes[2]
        return RING[x] + RING[y] + RING[z // 2]

    return sorted(range(sizes[0] * sizes[1] * sizes[2]), key=lambda q: (-hops(q), -q))


def flipped(place, mask):
    return [place, place + 1 - 2 * (place % 2), (place + 2) % 4, 3 - place][mask]


def iota_bf16(shape):
    return lax.broadcasted_iota(jnp.int32, shape, 0).astype(F32).astype(BF16)


def spread(row, count):
    return jnp.broadcast_to(row, (count, row.shape[1])).astype(BF16)


def one_hot(ids, row):
    return jnp.where(ids == spread(row, ids.shape[0]), jnp.ones((), BF16), jnp.zeros((), BF16))


def twice(ids):
    return jnp.concatenate([ids, ids], axis=1)


def chunk_at(step, g, group):
    return pl.ds(pl.multiple_of((step * group + g) * CHUNK, CHUNK), CHUNK)


def place(count, rank_ref, prefix_ref, ids_ref, block_ref, lane_ref):
    probes = rank_ref.shape[1]
    ids = twice(ids_ref[...])

    def body(step, carry):
        hots = [one_hot(ids, rank_ref[:, chunk_at(step, g, PLACED)].astype(F32)) for g in range(PLACED)]
        counted = jnp.dot(jnp.concatenate(hots, axis=0), prefix_ref[...], preferred_element_type=F32)
        for g in range(PLACED):
            at = chunk_at(step, g, PLACED)
            piece = counted[g * count : (g + 1) * count].astype(BF16)
            inside = piece[:, :CHUNK] + twice(carry)
            inside = jnp.where(hots[g] > jnp.zeros((), BF16), inside, jnp.zeros((), BF16))
            total = inside[:16]
            for k in range(1, count // 16):
                total = total + inside[16 * k : 16 * k + 16]
            position = jnp.sum(total.astype(F32), axis=0, keepdims=True) - 1.0
            block = jnp.floor(position * (1.0 / PIECE))
            lane_ref[:, at] = position - block * PIECE
            block_ref[:, at] = block
            carry = carry + piece[:, CHUNK:]
        return carry

    lax.fori_loop(0, probes // (CHUNK * PLACED), body, jnp.zeros((count, LANES), BF16))


def scatter(first, many, rank_ref, coords_ref, slot_ref, block_ref, lane_ref, ids_ref, send_ref, acc_ref):
    probes = rank_ref.shape[1]
    ids = twice(ids_ref[first : first + many, :])
    lane_ids = iota_bf16((PIECE, CHUNK))
    zero = jnp.zeros((), BF16)
    acc_ref[...] = jnp.zeros_like(acc_ref)

    def body(step, _):
        row_hots, lane_parts = [], []
        for g in range(GATHERED):
            at = chunk_at(step, g, GATHERED)
            rank, block, lane = rank_ref[:, at].astype(F32), block_ref[:, at], lane_ref[:, at]
            row_hots.append(
                jnp.concatenate(
                    [one_hot(ids, jnp.where(block == float(b), rank, -1.0)) for b in range(BLOCKS)], axis=0
                )
            )
            here = lane_ids == spread(lane, PIECE)
            high, low = [], []
            for v in range(3):
                value = coords_ref[v : v + 1, at]
                top = value.astype(BF16).astype(F32)
                high.append(top)
                low.append(value - top)
            high.append(slot_ref[:, at].astype(F32))
            chosen = [jnp.where(here, spread(part, PIECE), zero) for part in high + low]
            chosen.append(jnp.zeros((PIECE, CHUNK), BF16))
            lane_parts.append(jnp.concatenate(chosen, axis=0))
        acc_ref[...] += lax.dot_general(
            jnp.concatenate(row_hots, axis=1),
            jnp.concatenate(lane_parts, axis=1),
            (((1,), (1,)), ((), ())),
            preferred_element_type=F32,
        )
        return 0

    lax.fori_loop(0, probes // (GATHERED * CHUNK), body, 0)
    for b in range(BLOCKS):
        rows = slice(b * many, (b + 1) * many)
        send_ref[b, first : first + many, :] = acc_ref[rows, :LANES] + acc_ref[rows, LANES:]


def swap_groups(rows):
    lane = lax.broadcasted_iota(jnp.int32, (8, LANES), 1)
    for width in (2, 1):
        shift = width * PIECE
        lower = (lane // shift) % 2 == 0
        swapped = list(rows)
        for k in range(4):
            if (k // width) % 2 == 0:
                a, b = rows[k], rows[k + width]
                swapped[k] = jnp.where(lower, a, pltpu.roll(b, shift, 1))
                swapped[k + width] = jnp.where(lower, pltpu.roll(a, LANES - shift, 1), b)
        rows = swapped
    return rows


def lagrange(coord, nodes_ref):
    weight = nodes_ref[0:8, :]
    spread_coord = jnp.broadcast_to(coord, (8, LANES))
    for k in range(1, 8):
        weight = weight * (spread_coord - nodes_ref[8 * k : 8 * k + 8, :])
    return weight


def interpolate(rows, fields_ref, nodes_ref, pickers):
    depth = fields_ref.shape[1]
    elements = depth // 8
    zero = jnp.zeros((), BF16)
    ids = iota_bf16((16, LANES))
    pieces = [[] for _ in range(4)]
    for pair in range(len(rows[0]) // 2):
        picker_ref = pickers[pair % len(pickers)]
        weights = []
        for j in range(2):
            r, s, t, slot = [row[2 * pair + j : 2 * pair + j + 1, :] for row in rows]
            weights.append((lagrange(r, nodes_ref), lagrange(s, nodes_ref)))
            weight_t = lagrange(t, nodes_ref)
            columns = slice(j * LANES, (j + 1) * LANES)
            masks = [ids == spread(slot - float(16 * k), 16) for k in range(elements // 16)]
            for c in range(8):
                weight = spread(weight_t[c : c + 1, :], 16)
                for k in range(elements // 16):
                    at = c * elements + k * 16
                    picker_ref[at : at + 16, columns] = jnp.where(masks[k], weight, zero)
        along = jnp.dot(fields_ref[...], picker_ref[...], preferred_element_type=F32)
        for j in range(2):
            weight_r, weight_s = weights[j]
            columns = slice(j * LANES, (j + 1) * LANES)
            factors = [jnp.broadcast_to(weight_r[a : a + 1, :], (8, LANES)) for a in range(8)]
            for f in range(4):
                total = along[f * 64 : f * 64 + 8, columns] * factors[0]
                for a in range(1, 8):
                    total += along[f * 64 + a * 8 : f * 64 + a * 8 + 8, columns] * factors[a]
                pieces[f].append(jnp.sum(total * weight_s, axis=0, keepdims=True))
    return [jnp.concatenate(piece, axis=0) for piece in pieces]


def sample_kernel(
    sizes,
    rank_ref,
    coords_ref,
    slot_ref,
    prefix_ref,
    order_ref,
    fields_ref,
    nodes_ref,
    back_ref,
    block_ref,
    lane_ref,
    ids_ref,
    acc_ref,
    send_ref,
    recv_ref,
    values_ref,
    picker_a,
    picker_b,
    out_sem,
    in_sem,
    back_out_sem,
    back_in_sem,
):
    count = sizes[0] * sizes[1] * sizes[2]
    last = count - 1
    gx, gy, gz = [lax.axis_index(axis) for axis in AXES]
    me = (gx * sizes[1] + gy) * sizes[2] + gz
    order = far_to_near(sizes)
    xs, ys, zs = [[flipped(place, m) for m in range(4)] for place in (gx, gy, gz // 2)]
    cores = [gz % 2, 1 - gz % 2]
    mesh_ids = pl.DeviceIdType.MESH

    def peer(i):
        q = order[i]
        z = q % sizes[2]
        return (xs[q // (sizes[1] * sizes[2])], ys[(q // sizes[2]) % sizes[1]], zs[z // 2] * 2 + cores[z % 2])

    def remote(source, target, sent, arrived, i, device):
        return pltpu.make_async_remote_copy(
            src_ref=source.at[:, i],
            dst_ref=target.at[:, i],
            send_sem=sent.at[i],
            recv_sem=arrived.at[i],
            device_id=device,
            device_id_type=mesh_ids,
        )

    def outward(i, device):
        return remote(send_ref, recv_ref, out_sem, in_sem, i, device)

    def backward(i, device):
        return remote(values_ref, back_ref, back_out_sem, back_in_sem, i, device)

    here = (gx, gy, gz)
    barrier = pltpu.get_barrier_semaphore()
    for i in range(last):
        pl.semaphore_signal(barrier, inc=1, device_id=peer(i), device_id_type=mesh_ids)
    ids_ref[...] = jnp.bitwise_xor(order_ref[...], me).astype(F32).astype(BF16)
    place(count, rank_ref, prefix_ref, ids_ref, block_ref, lane_ref)
    half = count // 2
    for part in range(2):
        scatter(
            part * half, half, rank_ref, coords_ref, slot_ref, block_ref, lane_ref, ids_ref, send_ref, acc_ref
        )
        if part == 0:
            pl.semaphore_wait(barrier, last)
        for i in range(part * half, min((part + 1) * half, last)):
            outward(i, peer(i)).start()
    for b in range(BLOCKS):
        recv_ref[b, last : last + 1, :] = send_ref[b, last : last + 1, :]

    def body(step, _):
        quad, turn = step // 5, step % 5
        tail = turn // 4
        octet = quad * 4 + turn
        base = (1 - tail) * (octet * 8) + tail * (quad * 32)
        for j in range(8):

            @pl.when((1 - tail) * (octet * 8 + j) + tail * last < last)
            def _():
                outward(octet * 8 + j, here).wait_recv()

        spots = []
        for m in range(4):
            row = pl.multiple_of(base + tail * (8 * m), 8)
            spots.append((m * (1 - tail) + 4 * tail, pl.ds(row, 8)))
        rows = swap_groups([recv_ref[b, at, :] for b, at in spots])
        values = swap_groups(interpolate(rows, fields_ref, nodes_ref, [picker_a, picker_b]))
        for (b, at), value in zip(spots, values):
            values_ref[b, at, :] = value

        for g in range(count // 32):

            @pl.when(step == 5 * g + 4)
            def _():
                for i in range(32 * g, min(32 * g + 32, last)):
                    backward(i, peer(i)).start()

        return 0

    lax.fori_loop(0, count // 32 * 5, body, 0)
    for b in range(BLOCKS):
        back_ref[b, last : last + 1, :] = values_ref[b, last : last + 1, :]

    def finish(i, _):
        outward(i, here).wait_send()
        backward(i, here).wait()
        return 0

    lax.fori_loop(0, last, finish, 0)


def return_kernel(values_ref, rank_ref, block_ref, lane_ref, ids_ref, out_ref, table_ref):
    probes = rank_ref.shape[1]
    count = values_ref.shape[1]
    for b in range(BLOCKS):
        table_ref[:, b * count : (b + 1) * count] = values_ref[b].T.astype(BF16)
    ids = twice(ids_ref[...])
    lane_ids = lax.broadcasted_iota(jnp.int32, (PIECE, CHUNK), 0).astype(F32)

    def body(step, _):
        for g in range(4):
            at = chunk_at(step, g, 4)
            rank, block = rank_ref[:, at].astype(F32), block_ref[:, at]
            hot = jnp.concatenate(
                [one_hot(ids, jnp.where(block == float(b), rank, -1.0)) for b in range(BLOCKS)], axis=0
            )
            picked = jnp.dot(table_ref[...], hot, preferred_element_type=F32)
            here = lane_ids == jnp.broadcast_to(lane_ref[:, at], (PIECE, CHUNK))
            for f in range(4):
                out_ref[f : f + 1, at] = jnp.sum(
                    jnp.where(here, picked[f * PIECE : (f + 1) * PIECE], 0.0), axis=0, keepdims=True
                )
        return 0

    lax.fori_loop(0, probes // (4 * CHUNK), body, 0)


VMEM = pl.BlockSpec(memory_space=pltpu.VMEM)


def call(kernel, inputs, outputs, scratch, **options):
    return pl.pallas_call(
        kernel,
        out_shape=outputs,
        in_specs=[VMEM] * inputs,
        out_specs=jax.tree.map(lambda _: VMEM, outputs),
        scratch_shapes=scratch,
        compiler_params=pltpu.CompilerParams(vmem_limit_bytes=48 << 20, **options),
    )


def local(sizes, fields, coordinates, element_rank, element_slot):
    count = sizes[0] * sizes[1] * sizes[2]
    probes = element_slot.shape[0]
    elements = fields.shape[0]
    layout = jax.ShapeDtypeStruct((BLOCKS, count, LANES), F32)
    line = jax.ShapeDtypeStruct((1, probes), F32)

    lower = np.arange(CHUNK)
    prefix = np.concatenate([lower[:, None] <= lower[None, :], np.ones((CHUNK, LANES))], axis=1)
    order = np.broadcast_to(np.array(far_to_near(sizes), np.int32)[:, None], (count, LANES))
    turned = fields.reshape(elements, 256, 8).transpose(1, 2, 0).reshape(256, 8 * elements)
    nodes = jnp.broadcast_to(jnp.asarray(node_table, F32), (64, LANES))
    picker = pltpu.VMEM((8 * elements, 2 * LANES), BF16)
    buffer = pltpu.VMEM(layout.shape, F32)
    arrivals = pltpu.SemaphoreType.DMA((count,))
    rank = element_rank.reshape(1, probes)
    returned, block, lane, ids = call(
        functools.partial(sample_kernel, sizes),
        7,
        (layout, line, line, jax.ShapeDtypeStruct((count, LANES), BF16)),
        [pltpu.VMEM((BLOCKS * count // 2, 2 * LANES), F32)] + [buffer] * 3 + [picker] * 2 + [arrivals] * 4,
        collective_id=0,
        has_side_effects=True,
    )(
        rank,
        coordinates,
        element_slot.reshape(1, probes),
        jnp.asarray(prefix, BF16),
        jnp.asarray(order),
        turned,
        nodes,
    )
    return call(
        return_kernel,
        5,
        jax.ShapeDtypeStruct((4, probes), F32),
        [pltpu.VMEM((LANES, count * BLOCKS), BF16)],
    )(returned, rank, block, lane, ids)


def solution(mesh):
    sizes = tuple(mesh.shape[axis] for axis in AXES)
    placed = (P(AXES, None), P(None, AXES), P(AXES, None), P(AXES))
    return jax.shard_map(
        functools.partial(local, sizes),
        mesh=mesh,
        in_specs=placed,
        out_specs=P(None, AXES),
        check_vma=False,
    )
```

time: 84 us -> 68.7 us (0.82)
  Pallas kernels: 81.4 us -> 65.8 us
    pallas_call x2, Pallas kernels: 81.4 us -> 65.8 us  [the longest x1 58.8 us: local(): call(functools.partial(sample_kernel, sizes), 7, (layout, line, line, jax...]
    unnamed x12 -> x14, local copies, waits for them, and re-layouts: 2.23 us -> 2.51 us
where the time goes in v1:
time: 68.7 us; the launch traced here: 68.5 us
  Pallas kernels  65.8 us (96%)
  local copies, waits for them, and re-layouts  2.66 us (4%)
    pallas_call x1, Pallas kernels, local(): call(functools.partial(sample_kernel, sizes), 7, (layout, line, line, jax...  58.8 us
    pallas_call x1, Pallas kernels, local(): call(return_kernel, 5, jax.ShapeDtypeStruct((4, probes), F32), [pltpu.VME...  7.04 us
    unnamed x14, local copies, waits for them, and re-layouts  2.51 us

profile of v1, /device:TPU:1, one launch (start us, length us, event | category | flops | bytes accessed | tf_op | source)
XLA Modules:
  0.0 68.5 jit_solution(13493300241717108305)
XLA Ops:
  0.0 1.3 %copy.9 = bf16[128,2048]{0,1:T(8,128)(2,1)S(1)} copy(bf16[128,2048]{1,0:T(8,128)(2,1)} %param.7) | data formatting | bytes 1048576 | tf_op args[0]
  1.3 0.0 copy-start.4
  1.3 0.0 copy-start
  1.3 0.0 copy-start.2
  1.4 0.0 copy-start.3
  1.4 0.1 copy.12
  1.5 0.0 copy-start.1
  1.5 0.5 copy-done.4
  2.0 0.0 copy-start.5
  2.0 0.1 jit_solution_.3.order_ref
  2.1 0.6 copy-done.5
  2.6 0.1 broadcast_in_dim.8.nodes_ref
  2.7 0.0 copy-done
  2.7 0.0 copy-done.2
  2.7 0.0 copy-done.3
  2.7 0.0 copy-done.1
  2.7 58.8 %shard_map.73 = (f32[5,128,128]{2,1,0:T(8,128)S(1)}, f32[1,16384]{1,0:T(1,128)S(1)}, f32[1,16384]{1,0:T(1,128)S(1)}, bf16[128,128]{1,0:T(8,128)(2,1)S(1)}) custom-call(s32[1,16384]{1,0:T(1,128)S(1)} %bitcast.10, f32[3,16384]{1,0:T(4,128)S(1)} %copy-done, s32[1,16384]{1,0:T(1,128)S(1)} %bitcast.12, bf16[256,384]{1,0:T(8,128)(2,1)S(1)} %copy-done.2, ...), custom_call_target="tpu_custom_call" | custom-call | tf_op jit(solution)/shard_map/pallas_call | solution.py:366
  61.5 7.0 %shard_map.74 = f32[4,16384]{1,0:T(4,128)} custom-call(f32[5,128,128]{2,1,0:T(8,128)S(1)} %get-tuple-element.9.values_ref, s32[1,16384]{1,0:T(1,128)S(1)} %bitcast.11, f32[1,16384]{1,0:T(1,128)S(1)} %get-tuple-element.10.block_ref, f32[1,16384]{1,0:T(1,128)S(1)} %get-tuple-element.11.lane_ref, bf16[128,128]{1,0:T(8,128)(2,1)S(1)} %get-tuple-element.12.ids_ref), custom_call_target="tpu_custom_call" | custom-call | tf_op jit(solution)/shard_map/pallas_call | solution.py:382
Async XLA Ops:
  1.3 0.7 copy-start.4
  1.3 1.4 %copy-start = (f32[3,16384]{1,0:T(4,128)S(1)}, f32[3,16384]{1,0:T(4,128)}, u32[]{:S(2)}) copy-start(f32[3,16384]{1,0:T(4,128)} %coords_ref.1) | copy-start | bytes 589828
  1.3 1.4 %copy-start.2 = (bf16[256,384]{1,0:T(8,128)(2,1)S(1)}, bf16[256,384]{1,0:T(8,128)(2,1)}, u32[]{:S(2)}) copy-start(bf16[256,384]{1,0:T(8,128)(2,1)} %constant.7.clone.prefix_ref) | copy-start | bytes 589828
  1.4 1.4 %copy-start.3 = (s32[16384]{0:T(1024)S(1)}, s32[16384]{0:T(1024)}, u32[]{:S(2)}) copy-start(s32[16384]{0:T(1024)} %param.10) | copy-start | bytes 196612
  1.5 1.3 %copy-start.1 = (s32[16384,1]{0,1:T(1,128)S(1)}, s32[16384,1]{0,1:T(1,128)}, u32[]{:S(2)}) copy-start(s32[16384,1]{0,1:T(1,128)} %param.9) | copy-start | bytes 196612
  2.0 0.7 copy-start.5

commit v2 on v1

--- a/solution.py
+++ b/solution.py
@@ -14,8 +14,9 @@
 CHUNK = 256
 PIECE = 32
 BLOCKS = 5
-PLACED = 8
-GATHERED = 4
+PLACED = 16
+GATHERED = 16
+RETURNED = 16
 
 gll_points = np.array(
     [
@@ -161,27 +162,26 @@
     return weight
 
 
-def interpolate(rows, fields_ref, nodes_ref, pickers):
+def interpolate(rows, fields_ref, nodes_ref):
     depth = fields_ref.shape[1]
     elements = depth // 8
     zero = jnp.zeros((), BF16)
     ids = iota_bf16((16, LANES))
     pieces = [[] for _ in range(4)]
     for pair in range(len(rows[0]) // 2):
-        picker_ref = pickers[pair % len(pickers)]
-        weights = []
+        weights, columns_of = [], []
         for j in range(2):
             r, s, t, slot = [row[2 * pair + j : 2 * pair + j + 1, :] for row in rows]
             weights.append((lagrange(r, nodes_ref), lagrange(s, nodes_ref)))
             weight_t = lagrange(t, nodes_ref)
-            columns = slice(j * LANES, (j + 1) * LANES)
-            masks = [ids == spread(slot - float(16 * k), 16) for k in range(elements // 16)]
-            for c in range(8):
-                weight = spread(weight_t[c : c + 1, :], 16)
-                for k in range(elements // 16):
-                    at = c * elements + k * 16
-                    picker_ref[at : at + 16, columns] = jnp.where(masks[k], weight, zero)
-        along = jnp.dot(fields_ref[...], picker_ref[...], preferred_element_type=F32)
+            spread_t = [spread(weight_t[c : c + 1, :], 16) for c in range(8)]
+            hots = [
+                jnp.where(ids == spread(slot - float(16 * k), 16), jnp.ones((), BF16), zero)
+                for k in range(elements // 16)
+            ]
+            columns_of.append(jnp.concatenate([hot * weight for weight in spread_t for hot in hots], axis=0))
+        picker = jnp.concatenate(columns_of, axis=1)
+        along = jnp.dot(fields_ref[...], picker, preferred_element_type=F32)
         for j in range(2):
             weight_r, weight_s = weights[j]
             columns = slice(j * LANES, (j + 1) * LANES)
@@ -211,8 +211,6 @@
     send_ref,
     recv_ref,
     values_ref,
-    picker_a,
-    picker_b,
     out_sem,
     in_sem,
     back_out_sem,
@@ -266,36 +264,33 @@
     for b in range(BLOCKS):
         recv_ref[b, last : last + 1, :] = send_ref[b, last : last + 1, :]
 
-    def body(step, _):
-        quad, turn = step // 5, step % 5
-        tail = turn // 4
-        octet = quad * 4 + turn
-        base = (1 - tail) * (octet * 8) + tail * (quad * 32)
-        for j in range(8):
-
-            @pl.when((1 - tail) * (octet * 8 + j) + tail * last < last)
+    def body(quad, _):
+        for j in range(32):
+
+            @pl.when(quad * 32 + j < last)
             def _():
-                outward(octet * 8 + j, here).wait_recv()
-
-        spots = []
-        for m in range(4):
-            row = pl.multiple_of(base + tail * (8 * m), 8)
-            spots.append((m * (1 - tail) + 4 * tail, pl.ds(row, 8)))
-        rows = swap_groups([recv_ref[b, at, :] for b, at in spots])
-        values = swap_groups(interpolate(rows, fields_ref, nodes_ref, [picker_a, picker_b]))
-        for (b, at), value in zip(spots, values):
-            values_ref[b, at, :] = value
+                outward(quad * 32 + j, here).wait_recv()
+
+        for turn in range(5):
+            spots = []
+            for m in range(4):
+                row = pl.multiple_of(quad * 32 + 8 * (turn if turn < 4 else m), 8)
+                spots.append((m if turn < 4 else 4, pl.ds(row, 8)))
+            rows = swap_groups([recv_ref[b, at, :] for b, at in spots])
+            values = swap_groups(interpolate(rows, fields_ref, nodes_ref))
+            for (b, at), value in zip(spots, values):
+                values_ref[b, at, :] = value
 
         for g in range(count // 32):
 
-            @pl.when(step == 5 * g + 4)
+            @pl.when(quad == g)
             def _():
                 for i in range(32 * g, min(32 * g + 32, last)):
                     backward(i, peer(i)).start()
 
         return 0
 
-    lax.fori_loop(0, count // 32 * 5, body, 0)
+    lax.fori_loop(0, count // 32, body, 0)
     for b in range(BLOCKS):
         back_ref[b, last : last + 1, :] = values_ref[b, last : last + 1, :]
 
@@ -316,8 +311,8 @@
     lane_ids = lax.broadcasted_iota(jnp.int32, (PIECE, CHUNK), 0).astype(F32)
 
     def body(step, _):
-        for g in range(4):
-            at = chunk_at(step, g, 4)
+        for g in range(RETURNED):
+            at = chunk_at(step, g, RETURNED)
             rank, block = rank_ref[:, at].astype(F32), block_ref[:, at]
             hot = jnp.concatenate(
                 [one_hot(ids, jnp.where(block == float(b), rank, -1.0)) for b in range(BLOCKS)], axis=0
@@ -330,7 +325,7 @@
                 )
         return 0
 
-    lax.fori_loop(0, probes // (4 * CHUNK), body, 0)
+    lax.fori_loop(0, probes // (RETURNED * CHUNK), body, 0)
 
 
 VMEM = pl.BlockSpec(memory_space=pltpu.VMEM)
@@ -359,7 +354,6 @@
     order = np.broadcast_to(np.array(far_to_near(sizes), np.int32)[:, None], (count, LANES))
     turned = fields.reshape(elements, 256, 8).transpose(1, 2, 0).reshape(256, 8 * elements)
     nodes = jnp.broadcast_to(jnp.asarray(node_table, F32), (64, LANES))
-    picker = pltpu.VMEM((8 * elements, 2 * LANES), BF16)
     buffer = pltpu.VMEM(layout.shape, F32)
     arrivals = pltpu.SemaphoreType.DMA((count,))
     rank = element_rank.reshape(1, probes)
@@ -367,7 +361,7 @@
         functools.partial(sample_kernel, sizes),
         7,
         (layout, line, line, jax.ShapeDtypeStruct((count, LANES), BF16)),
-        [pltpu.VMEM((BLOCKS * count // 2, 2 * LANES), F32)] + [buffer] * 3 + [picker] * 2 + [arrivals] * 4,
+        [pltpu.VMEM((BLOCKS * count // 2, 2 * LANES), F32)] + [buffer] * 3 + [arrivals] * 4,
         collective_id=0,
         has_side_effects=True,
     )(

time: 68.7 us -> 49.7 us (0.72)
  Pallas kernels: 65.8 us -> 46.8 us
    pallas_call x1, Pallas kernels: 58.8 us -> 41.9 us  [local(): call(functools.partial(sample_kernel, sizes), 7, (layout, line, line, jax...]
    pallas_call x1, Pallas kernels: 7.04 us -> 4.92 us  [local(): call(return_kernel, 5, jax.ShapeDtypeStruct((4, probes), F32), [pltpu.VME...]
where the time goes in v2:
time: 49.7 us; the launch traced here: 49.6 us
  Pallas kernels  46.8 us (94%)
  local copies, waits for them, and re-layouts  2.66 us (5%)
    pallas_call x1, Pallas kernels, local(): call(functools.partial(sample_kernel, sizes), 7, (layout, line, line, jax...  41.9 us
    pallas_call x1, Pallas kernels, local(): call(return_kernel, 5, jax.ShapeDtypeStruct((4, probes), F32), [pltpu.VME...  4.92 us
    unnamed x14, local copies, waits for them, and re-layouts  2.51 us

profile of v2, /device:TPU:1, one launch (start us, length us, event | category | flops | bytes accessed | tf_op | source)
XLA Modules:
  0.0 49.6 jit_solution(18029945457075345280)
XLA Ops:
  0.0 1.3 %copy.9 = bf16[128,2048]{0,1:T(8,128)(2,1)S(1)} copy(bf16[128,2048]{1,0:T(8,128)(2,1)} %param.7) | data formatting | bytes 1048576 | tf_op args[0]
  1.3 0.0 copy-start.4
  1.3 0.0 copy-start
  1.3 0.0 copy-start.2
  1.4 0.0 copy-start.3
  1.4 0.1 copy.12
  1.5 0.0 copy-start.1
  1.5 0.5 %copy-done.4 = s32[128]{0:T(128)S(1)} copy-done((s32[128]{0:T(128)S(1)}, s32[128]{0:T(128)}, u32[]{:S(2)}) %copy-start.4) | copy-done | bytes 536
  2.0 0.0 copy-start.5
  2.0 0.1 jit_solution_.3.order_ref
  2.1 0.6 %copy-done.5 = f32[64]{0:T(128)S(1)} copy-done((f32[64]{0:T(128)S(1)}, f32[64]{0:T(128)}, u32[]{:S(2)}) %copy-start.5) | copy-done | bytes 280
  2.6 0.1 broadcast_in_dim.8.nodes_ref
  2.7 0.0 copy-done
  2.7 0.0 copy-done.2
  2.7 0.0 copy-done.3
  2.7 0.0 copy-done.1
  2.7 41.9 %shard_map.73 = (f32[5,128,128]{2,1,0:T(8,128)S(1)}, f32[1,16384]{1,0:T(1,128)S(1)}, f32[1,16384]{1,0:T(1,128)S(1)}, bf16[128,128]{1,0:T(8,128)(2,1)S(1)}) custom-call(s32[1,16384]{1,0:T(1,128)S(1)} %bitcast.10, f32[3,16384]{1,0:T(4,128)S(1)} %copy-done, s32[1,16384]{1,0:T(1,128)S(1)} %bitcast.12, bf16[256,384]{1,0:T(8,128)(2,1)S(1)} %copy-done.2, ...), custom_call_target="tpu_custom_call" | custom-call | tf_op jit(solution)/shard_map/pallas_call | solution.py:360
  44.6 4.9 %shard_map.74 = f32[4,16384]{1,0:T(4,128)} custom-call(f32[5,128,128]{2,1,0:T(8,128)S(1)} %get-tuple-element.9.values_ref, s32[1,16384]{1,0:T(1,128)S(1)} %bitcast.11, f32[1,16384]{1,0:T(1,128)S(1)} %get-tuple-element.10.block_ref, f32[1,16384]{1,0:T(1,128)S(1)} %get-tuple-element.11.lane_ref, bf16[128,128]{1,0:T(8,128)(2,1)S(1)} %get-tuple-element.12.ids_ref), custom_call_target="tpu_custom_call" | custom-call | tf_op jit(solution)/shard_map/pallas_call | solution.py:376
Async XLA Ops:
  1.3 0.7 %copy-start.4 = (s32[128]{0:T(128)S(1)}, s32[128]{0:T(128)}, u32[]{:S(2)}) copy-start(s32[128]{0:T(128)} %constant.8.clone) | copy-start | bytes 1540
  1.3 1.4 %copy-start = (f32[3,16384]{1,0:T(4,128)S(1)}, f32[3,16384]{1,0:T(4,128)}, u32[]{:S(2)}) copy-start(f32[3,16384]{1,0:T(4,128)} %coords_ref.1) | copy-start | bytes 589828
  1.3 1.4 %copy-start.2 = (bf16[256,384]{1,0:T(8,128)(2,1)S(1)}, bf16[256,384]{1,0:T(8,128)(2,1)}, u32[]{:S(2)}) copy-start(bf16[256,384]{1,0:T(8,128)(2,1)} %constant.7.clone.prefix_ref) | copy-start | bytes 589828
  1.4 1.4 %copy-start.3 = (s32[16384]{0:T(1024)S(1)}, s32[16384]{0:T(1024)}, u32[]{:S(2)}) copy-start(s32[16384]{0:T(1024)} %param.10) | copy-start | bytes 196612
  1.5 1.3 %copy-start.1 = (s32[16384,1]{0,1:T(1,128)S(1)}, s32[16384,1]{0,1:T(1,128)}, u32[]{:S(2)}) copy-start(s32[16384,1]{0,1:T(1,128)} %param.9) | copy-start | bytes 196612
  2.0 0.7 %copy-start.5 = (f32[64]{0:T(128)S(1)}, f32[64]{0:T(128)}, u32[]{:S(2)}) copy-start(f32[64]{0:T(128)} %constant.9) | copy-start | bytes 772

commit v3 on v2

--- a/solution.py
+++ b/solution.py
@@ -33,19 +33,18 @@
 gll_scale = np.array(
     [1.0 / np.prod([gll_points[a] - gll_points[b] for b in range(8) if b != a]) for a in range(8)]
 )
-node_table = np.stack(
-    [gll_scale] + [np.roll(gll_points, -k) for k in range(1, 8)], axis=0
-).reshape(64, 1)
+node_table = np.stack([gll_scale] + [np.roll(gll_points, -k) for k in range(1, 8)], axis=0)
 
 RING = [0, 1, 2, 1]
 
 
-def far_to_near(sizes):
+def served(sizes):
     def hops(q):
         x, y, z = q // (sizes[1] * sizes[2]), (q // sizes[2]) % sizes[1], q % sizes[2]
         return RING[x] + RING[y] + RING[z // 2]
 
-    return sorted(range(sizes[0] * sizes[1] * sizes[2]), key=lambda q: (-hops(q), -q))
+    far = sorted(range(sizes[0] * sizes[1] * sizes[2]), key=lambda q: (-hops(q), -q))
+    return far[96:] + far[:32] + far[32:96]
 
 
 def flipped(place, mask):
@@ -72,18 +71,19 @@
     return pl.ds(pl.multiple_of((step * group + g) * CHUNK, CHUNK), CHUNK)
 
 
-def place(count, rank_ref, prefix_ref, ids_ref, block_ref, lane_ref):
+def place(count, rank_ref, ids_ref, block_ref, lane_ref):
     probes = rank_ref.shape[1]
     ids = twice(ids_ref[...])
+    before = lax.broadcasted_iota(jnp.int32, (CHUNK, CHUNK), 0) <= lax.broadcasted_iota(jnp.int32, (CHUNK, CHUNK), 1)
+    prefix = jnp.where(before, 1.0, 0.0).astype(BF16)
 
     def body(step, carry):
         hots = [one_hot(ids, rank_ref[:, chunk_at(step, g, PLACED)].astype(F32)) for g in range(PLACED)]
-        counted = jnp.dot(jnp.concatenate(hots, axis=0), prefix_ref[...], preferred_element_type=F32)
+        counted = jnp.dot(jnp.concatenate(hots, axis=0), prefix, preferred_element_type=F32)
         for g in range(PLACED):
             at = chunk_at(step, g, PLACED)
             piece = counted[g * count : (g + 1) * count].astype(BF16)
-            inside = piece[:, :CHUNK] + twice(carry)
-            inside = jnp.where(hots[g] > jnp.zeros((), BF16), inside, jnp.zeros((), BF16))
+            inside = (piece + twice(carry)) * hots[g]
             total = inside[:16]
             for k in range(1, count // 16):
                 total = total + inside[16 * k : 16 * k + 16]
@@ -91,7 +91,7 @@
             block = jnp.floor(position * (1.0 / PIECE))
             lane_ref[:, at] = position - block * PIECE
             block_ref[:, at] = block
-            carry = carry + piece[:, CHUNK:]
+            carry = carry + jnp.broadcast_to(piece[:, CHUNK - 1 :], carry.shape)
         return carry
 
     lax.fori_loop(0, probes // (CHUNK * PLACED), body, jnp.zeros((count, LANES), BF16))
@@ -152,6 +152,23 @@
                 swapped[k + width] = jnp.where(lower, pltpu.roll(a, LANES - shift, 1), b)
         rows = swapped
     return rows
+
+
+def write_nodes(nodes_ref):
+    row = lax.broadcasted_iota(jnp.int32, (8, LANES), 0)
+    for k in range(8):
+        value = jnp.full((8, LANES), float(node_table[k, 0]), F32)
+        for a in range(1, 8):
+            value = jnp.where(row == a, float(node_table[k, a]), value)
+        nodes_ref[8 * k : 8 * k + 8, :] = value
+
+
+def turn_fields(fields_ref, spaced_ref, turned_ref):
+    elements = fields_ref.shape[0]
+    for k in range(fields_ref.shape[1] // LANES):
+        spaced_ref[k * LANES : (k + 1) * LANES, :] = fields_ref[:, k * LANES : (k + 1) * LANES].astype(F32).T
+    for c in range(8):
+        turned_ref[:, c * elements : (c + 1) * elements] = spaced_ref[pl.ds(c, 256, stride=8), :].astype(BF16)
 
 
 def lagrange(coord, nodes_ref):
@@ -196,31 +213,38 @@
 
 def sample_kernel(
     sizes,
-    rank_ref,
-    coords_ref,
-    slot_ref,
-    prefix_ref,
-    order_ref,
-    fields_ref,
-    nodes_ref,
-    back_ref,
+    rank_hbm,
+    coords_hbm,
+    slot_hbm,
+    fields_hbm,
+    part_ref,
+    late_ref,
     block_ref,
     lane_ref,
     ids_ref,
     acc_ref,
+    spaced_ref,
+    turned_ref,
+    table_ref,
+    nodes_ref,
+    rank_ref,
+    coords_ref,
+    slot_ref,
+    fields_ref,
+    back_ref,
     send_ref,
     recv_ref,
     values_ref,
+    load_sem,
     out_sem,
     in_sem,
     back_out_sem,
     back_in_sem,
 ):
     count = sizes[0] * sizes[1] * sizes[2]
-    last = count - 1
+    order = served(sizes)
+    own, quads = order.index(0), count // 32
     gx, gy, gz = [lax.axis_index(axis) for axis in AXES]
-    me = (gx * sizes[1] + gy) * sizes[2] + gz
-    order = far_to_near(sizes)
     xs, ys, zs = [[flipped(place, m) for m in range(4)] for place in (gx, gy, gz // 2)]
     cores = [gz % 2, 1 - gz % 2]
     mesh_ids = pl.DeviceIdType.MESH
@@ -246,28 +270,49 @@
     def backward(i, device):
         return remote(values_ref, back_ref, back_out_sem, back_in_sem, i, device)
 
+    loads = [
+        pltpu.make_async_copy(source, target, load_sem.at[k])
+        for k, (source, target) in enumerate(
+            [(rank_hbm, rank_ref), (coords_hbm, coords_ref), (slot_hbm, slot_ref), (fields_hbm, fields_ref)]
+        )
+    ]
+    for load in loads:
+        load.start()
     here = (gx, gy, gz)
     barrier = pltpu.get_barrier_semaphore()
-    for i in range(last):
+    for i in range(count):
+        if i == own:
+            continue
         pl.semaphore_signal(barrier, inc=1, device_id=peer(i), device_id_type=mesh_ids)
-    ids_ref[...] = jnp.bitwise_xor(order_ref[...], me).astype(F32).astype(BF16)
-    place(count, rank_ref, prefix_ref, ids_ref, block_ref, lane_ref)
+    for i in range(count):
+        x, y, z = peer(i)
+        place_of = (x * sizes[1] + y) * sizes[2] + z
+        spaced_ref[i : i + 1, :] = jnp.broadcast_to(place_of.astype(F32), (1, LANES))
+    ids_ref[...] = spaced_ref[:count, :].astype(BF16)
+    write_nodes(nodes_ref)
+    loads[0].wait()
+    place(count, rank_ref, ids_ref, block_ref, lane_ref)
+    loads[1].wait()
+    loads[2].wait()
     half = count // 2
     for part in range(2):
         scatter(
             part * half, half, rank_ref, coords_ref, slot_ref, block_ref, lane_ref, ids_ref, send_ref, acc_ref
         )
         if part == 0:
-            pl.semaphore_wait(barrier, last)
-        for i in range(part * half, min((part + 1) * half, last)):
-            outward(i, peer(i)).start()
+            pl.semaphore_wait(barrier, count - 1)
+        for i in range(part * half, (part + 1) * half):
+            if i != own:
+                outward(i, peer(i)).start()
     for b in range(BLOCKS):
-        recv_ref[b, last : last + 1, :] = send_ref[b, last : last + 1, :]
+        recv_ref[b, own : own + 1, :] = send_ref[b, own : own + 1, :]
+    loads[3].wait()
+    turn_fields(fields_ref, spaced_ref, turned_ref)
 
     def body(quad, _):
         for j in range(32):
 
-            @pl.when(quad * 32 + j < last)
+            @pl.when(quad * 32 + j != own)
             def _():
                 outward(quad * 32 + j, here).wait_recv()
 
@@ -277,65 +322,84 @@
                 row = pl.multiple_of(quad * 32 + 8 * (turn if turn < 4 else m), 8)
                 spots.append((m if turn < 4 else 4, pl.ds(row, 8)))
             rows = swap_groups([recv_ref[b, at, :] for b, at in spots])
-            values = swap_groups(interpolate(rows, fields_ref, nodes_ref))
+            values = swap_groups(interpolate(rows, turned_ref, nodes_ref))
             for (b, at), value in zip(spots, values):
                 values_ref[b, at, :] = value
 
-        for g in range(count // 32):
+        for g in range(quads):
 
             @pl.when(quad == g)
             def _():
-                for i in range(32 * g, min(32 * g + 32, last)):
-                    backward(i, peer(i)).start()
+                for i in range(32 * g, 32 * g + 32):
+                    if i != own:
+                        backward(i, peer(i)).start()
 
         return 0
 
-    lax.fori_loop(0, count // 32, body, 0)
+    lax.fori_loop(0, quads, body, 0)
     for b in range(BLOCKS):
-        back_ref[b, last : last + 1, :] = values_ref[b, last : last + 1, :]
+        back_ref[b, own : own + 1, :] = values_ref[b, own : own + 1, :]
 
     def finish(i, _):
-        outward(i, here).wait_send()
-        backward(i, here).wait()
+        @pl.when(i != own)
+        def _():
+            outward(i, here).wait_send()
+            backward(i, here).wait()
+
         return 0
 
-    lax.fori_loop(0, last, finish, 0)
-
-
-def return_kernel(values_ref, rank_ref, block_ref, lane_ref, ids_ref, out_ref, table_ref):
+    early = count - 32
+    lax.fori_loop(0, early, finish, 0)
+    rows = [back_ref[b, :early, :] for b in range(BLOCKS)]
+    rows.append(jnp.zeros((-BLOCKS * early % LANES, LANES), F32))
+    table_ref[...] = jnp.concatenate(rows, axis=0).T.astype(BF16)
+    pick(table_ref, ids_ref[:early, :], rank_ref, block_ref, lane_ref, None, part_ref)
+    lax.fori_loop(early, count, finish, 0)
+    for b in range(BLOCKS):
+        late_ref[b * 32 : (b + 1) * 32, :] = back_ref[b, early:, :]
+
+
+def pick(table_ref, ids, rank_ref, block_ref, lane_ref, part_ref, out_ref):
     probes = rank_ref.shape[1]
-    count = values_ref.shape[1]
-    for b in range(BLOCKS):
-        table_ref[:, b * count : (b + 1) * count] = values_ref[b].T.astype(BF16)
-    ids = twice(ids_ref[...])
+    ids = twice(ids)
     lane_ids = lax.broadcasted_iota(jnp.int32, (PIECE, CHUNK), 0).astype(F32)
 
     def body(step, _):
         for g in range(RETURNED):
             at = chunk_at(step, g, RETURNED)
             rank, block = rank_ref[:, at].astype(F32), block_ref[:, at]
-            hot = jnp.concatenate(
-                [one_hot(ids, jnp.where(block == float(b), rank, -1.0)) for b in range(BLOCKS)], axis=0
-            )
-            picked = jnp.dot(table_ref[...], hot, preferred_element_type=F32)
+            hots = [one_hot(ids, jnp.where(block == float(b), rank, -1.0)) for b in range(BLOCKS)]
+            spare = table_ref.shape[1] - BLOCKS * ids.shape[0]
+            if spare:
+                hots.append(jnp.zeros((spare, CHUNK), BF16))
+            picked = jnp.dot(table_ref[...], jnp.concatenate(hots, axis=0), preferred_element_type=F32)
             here = lane_ids == jnp.broadcast_to(lane_ref[:, at], (PIECE, CHUNK))
             for f in range(4):
-                out_ref[f : f + 1, at] = jnp.sum(
+                value = jnp.sum(
                     jnp.where(here, picked[f * PIECE : (f + 1) * PIECE], 0.0), axis=0, keepdims=True
                 )
+                out_ref[f : f + 1, at] = value if part_ref is None else value + part_ref[f : f + 1, at]
         return 0
 
     lax.fori_loop(0, probes // (RETURNED * CHUNK), body, 0)
 
 
+def return_kernel(late_ref, part_ref, rank_ref, block_ref, lane_ref, ids_ref, out_ref, table_ref):
+    late = late_ref.shape[0]
+    rows = jnp.concatenate([late_ref[...], jnp.zeros((-late % LANES, LANES), F32)], axis=0)
+    table_ref[...] = rows.T.astype(BF16)
+    pick(table_ref, ids_ref[-(late // BLOCKS) :, :], rank_ref, block_ref, lane_ref, part_ref, out_ref)
+
+
 VMEM = pl.BlockSpec(memory_space=pltpu.VMEM)
+HBM = pl.BlockSpec(memory_space=pltpu.HBM)
 
 
 def call(kernel, inputs, outputs, scratch, **options):
     return pl.pallas_call(
         kernel,
         out_shape=outputs,
-        in_specs=[VMEM] * inputs,
+        in_specs=inputs,
         out_specs=jax.tree.map(lambda _: VMEM, outputs),
         scratch_shapes=scratch,
         compiler_params=pltpu.CompilerParams(vmem_limit_bytes=48 << 20, **options),
@@ -346,39 +410,53 @@
     count = sizes[0] * sizes[1] * sizes[2]
     probes = element_slot.shape[0]
     elements = fields.shape[0]
-    layout = jax.ShapeDtypeStruct((BLOCKS, count, LANES), F32)
     line = jax.ShapeDtypeStruct((1, probes), F32)
 
-    lower = np.arange(CHUNK)
-    prefix = np.concatenate([lower[:, None] <= lower[None, :], np.ones((CHUNK, LANES))], axis=1)
-    order = np.broadcast_to(np.array(far_to_near(sizes), np.int32)[:, None], (count, LANES))
-    turned = fields.reshape(elements, 256, 8).transpose(1, 2, 0).reshape(256, 8 * elements)
-    nodes = jnp.broadcast_to(jnp.asarray(node_table, F32), (64, LANES))
-    buffer = pltpu.VMEM(layout.shape, F32)
+    buffer = pltpu.VMEM((BLOCKS, count, LANES), F32)
     arrivals = pltpu.SemaphoreType.DMA((count,))
     rank = element_rank.reshape(1, probes)
-    returned, block, lane, ids = call(
+    late = BLOCKS * 32
+    whole = jax.ShapeDtypeStruct((4, probes), F32)
+    part, returned, block, lane, ids = call(
         functools.partial(sample_kernel, sizes),
-        7,
-        (layout, line, line, jax.ShapeDtypeStruct((count, LANES), BF16)),
-        [pltpu.VMEM((BLOCKS * count // 2, 2 * LANES), F32)] + [buffer] * 3 + [arrivals] * 4,
+        [HBM] * 4,
+        (
+            whole,
+            jax.ShapeDtypeStruct((late, LANES), F32),
+            line,
+            line,
+            jax.ShapeDtypeStruct((count, LANES), BF16),
+        ),
+        [
+            pltpu.VMEM((BLOCKS * count // 2, 2 * LANES), F32),
+            pltpu.VMEM((256 * 8, elements), F32),
+            pltpu.VMEM((256, 8 * elements), BF16),
+            pltpu.VMEM((LANES, -(-BLOCKS * (count - 32) // LANES) * LANES), BF16),
+        ]
+        + [
+            pltpu.VMEM((64, LANES), F32),
+            pltpu.VMEM(rank.shape, jnp.int32),
+            pltpu.VMEM(coordinates.shape, F32),
+            pltpu.VMEM(rank.shape, jnp.int32),
+            pltpu.VMEM(fields.shape, BF16),
+        ]
+        + [buffer] * 4
+        + [pltpu.SemaphoreType.DMA((4,))]
+        + [arrivals] * 4,
         collective_id=0,
         has_side_effects=True,
     )(
-        rank,
-        coordinates,
-        element_slot.reshape(1, probes),
-        jnp.asarray(prefix, BF16),
-        jnp.asarray(order),
-        turned,
-        nodes,
+        *[
+            pltpu.with_memory_space_constraint(array, pltpu.HBM)
+            for array in (rank, coordinates, element_slot.reshape(1, probes), fields)
+        ]
     )
     return call(
         return_kernel,
-        5,
-        jax.ShapeDtypeStruct((4, probes), F32),
-        [pltpu.VMEM((LANES, count * BLOCKS), BF16)],
-    )(returned, rank, block, lane, ids)
+        [VMEM] * 6,
+        whole,
+        [pltpu.VMEM((LANES, -(-late // LANES) * LANES), BF16)],
+    )(returned, part, rank, block, lane, ids)
 
 
 def solution(mesh):

time: 49.7 us -> 44.5 us (0.90)
  local copies, waits for them, and re-layouts: 2.66 us -> 0.01 us
  Pallas kernels: 46.8 us -> 44.4 us
    unnamed x14 -> x2, local copies, waits for them, and re-layouts: 2.51 us -> 0.01 us
    pallas_call x2, Pallas kernels: 46.8 us -> 44.4 us  [the longest x1 41.5 us: local(): call(functools.partial(sample_kernel, sizes), [HBM] * 4, (whole, jax.Shap...]
where the time goes in v3:
time: 44.5 us; the launch traced here: 44.4 us
  Pallas kernels  44.4 us (100%)
    pallas_call x1, Pallas kernels, local(): call(functools.partial(sample_kernel, sizes), [HBM] * 4, (whole, jax.Shap...  41.5 us
    pallas_call x1, Pallas kernels, local(): call(return_kernel, [VMEM] * 6, whole, [pltpu.VMEM((LANES, -(-late // LAN...  2.94 us

profile of v3, /device:TPU:1, one launch (start us, length us, event | category | flops | bytes accessed | tf_op | source)
XLA Modules:
  0.0 44.4 jit_solution(664156899950721092)
XLA Ops:
  0.0 0.0 copy-start
  0.0 41.5 %shard_map.46 = (f32[4,16384]{1,0:T(4,128)S(1)}, f32[160,128]{1,0:T(8,128)S(1)}, f32[1,16384]{1,0:T(1,128)S(1)}, f32[1,16384]{1,0:T(1,128)S(1)}, bf16[128,128]{1,0:T(8,128)(2,1)S(1)}) custom-call(s32[1,16384]{1,0:T(1,128)} %bitcast.2, f32[3,16384]{1,0:T(4,128)} %coords_hbm.1, s32[1,16384]{1,0:T(1,128)} %bitcast.4, bf16[128,2048]{1,0:T(8,128)(2,1)} %fields_hbm.1), custom_call_target="tpu_custom_call" | custom-call | tf_op jit(solution)/shard_map/pallas_call | solution.py:420
  41.5 0.0 copy-done
  41.5 2.9 %shard_map.47 = f32[4,16384]{1,0:T(4,128)} custom-call(f32[160,128]{1,0:T(8,128)S(1)} %get-tuple-element.10.late_ref, f32[4,16384]{1,0:T(4,128)S(1)} %get-tuple-element.11.part_ref, s32[1,16384]{1,0:T(1,128)S(1)} %bitcast.3, f32[1,16384]{1,0:T(1,128)S(1)} %get-tuple-element.12.block_ref, f32[1,16384]{1,0:T(1,128)S(1)} %get-tuple-element.13.lane_ref, ...), custom_call_target="tpu_custom_call" | custom-call | tf_op jit(solution)/shard_map/pallas_call | solution.py:454
Async XLA Ops:
  0.0 41.5 %copy-start = (s32[16384,1]{0,1:T(1,128)S(1)}, s32[16384,1]{0,1:T(1,128)}, u32[]{:S(2)}) copy-start(s32[16384,1]{0,1:T(1,128)} %param.6) | copy-start | bytes 196612

commit v4 on v3

--- a/solution.py
+++ b/solution.py
@@ -14,6 +14,7 @@
 CHUNK = 256
 PIECE = 32
 BLOCKS = 5
+QUAD = 32
 PLACED = 16
 GATHERED = 16
 RETURNED = 16
@@ -35,20 +36,15 @@
 )
 node_table = np.stack([gll_scale] + [np.roll(gll_points, -k) for k in range(1, 8)], axis=0)
 
-RING = [0, 1, 2, 1]
+REACHED = ((0.0, 1.1, 1.2, 1.6), (0.0, 1.3, 1.5, 1.8), (0.0, 1.5, 2.3, 2.8))
 
 
 def served(sizes):
-    def hops(q):
-        x, y, z = q // (sizes[1] * sizes[2]), (q // sizes[2]) % sizes[1], q % sizes[2]
-        return RING[x] + RING[y] + RING[z // 2]
-
-    far = sorted(range(sizes[0] * sizes[1] * sizes[2]), key=lambda q: (-hops(q), -q))
-    return far[96:] + far[:32] + far[32:96]
-
-
-def flipped(place, mask):
-    return [place, place + 1 - 2 * (place % 2), (place + 2) % 4, 3 - place][mask]
+    def reached(rank):
+        x, y, z = rank // (sizes[1] * sizes[2]), (rank // sizes[2]) % sizes[1], rank % sizes[2] // 2
+        return REACHED[0][x] + REACHED[1][y] + REACHED[2][z]
+
+    return sorted(range(sizes[0] * sizes[1] * sizes[2]), key=lambda rank: (reached(rank), rank))
 
 
 def iota_bf16(shape):
@@ -242,33 +238,37 @@
     back_in_sem,
 ):
     count = sizes[0] * sizes[1] * sizes[2]
+    quads, half = count // QUAD, count // 2
+    me = (lax.axis_index("gx") * sizes[1] + lax.axis_index("gy")) * sizes[2] + lax.axis_index("gz")
     order = served(sizes)
-    own, quads = order.index(0), count // 32
-    gx, gy, gz = [lax.axis_index(axis) for axis in AXES]
-    xs, ys, zs = [[flipped(place, m) for m in range(4)] for place in (gx, gy, gz // 2)]
-    cores = [gz % 2, 1 - gz % 2]
+    own = jnp.int32(0)
+    for i in range(1, count):
+        own = jnp.where(me == order[i], i, own)
     mesh_ids = pl.DeviceIdType.MESH
 
     def peer(i):
-        q = order[i]
-        z = q % sizes[2]
-        return (xs[q // (sizes[1] * sizes[2])], ys[(q // sizes[2]) % sizes[1]], zs[z // 2] * 2 + cores[z % 2])
-
-    def remote(source, target, sent, arrived, i, device):
-        return pltpu.make_async_remote_copy(
+        rank = order[i]
+        return (rank // (sizes[1] * sizes[2]), (rank // sizes[2]) % sizes[1], rank % sizes[2])
+
+    def to_others(first, last, act):
+        for i in range(first, last):
+            pl.when(own != i)(functools.partial(act, i))
+
+    def send(source, target, sent, arrived, i):
+        pltpu.make_async_remote_copy(
             src_ref=source.at[:, i],
-            dst_ref=target.at[:, i],
-            send_sem=sent.at[i],
-            recv_sem=arrived.at[i],
-            device_id=device,
+            dst_ref=target.at[:, own],
+            send_sem=sent.at[0],
+            recv_sem=arrived.at[own // QUAD],
+            device_id=peer(i),
             device_id_type=mesh_ids,
-        )
-
-    def outward(i, device):
-        return remote(send_ref, recv_ref, out_sem, in_sem, i, device)
-
-    def backward(i, device):
-        return remote(values_ref, back_ref, back_out_sem, back_in_sem, i, device)
+        ).start()
+
+    def keep(source, target, arrived):
+        pltpu.make_async_copy(source.at[:, own], target.at[:, own], arrived.at[own // QUAD]).start()
+
+    def wait_for(many, buffer, sem):
+        pltpu.make_async_copy(buffer.at[:, :many], buffer.at[:, :many], sem).wait()
 
     loads = [
         pltpu.make_async_copy(source, target, load_sem.at[k])
@@ -278,48 +278,37 @@
     ]
     for load in loads:
         load.start()
-    here = (gx, gy, gz)
     barrier = pltpu.get_barrier_semaphore()
+    to_others(
+        0,
+        count,
+        lambda i: pl.semaphore_signal(barrier, inc=1, device_id=peer(i), device_id_type=mesh_ids),
+    )
     for i in range(count):
-        if i == own:
-            continue
-        pl.semaphore_signal(barrier, inc=1, device_id=peer(i), device_id_type=mesh_ids)
-    for i in range(count):
-        x, y, z = peer(i)
-        place_of = (x * sizes[1] + y) * sizes[2] + z
-        spaced_ref[i : i + 1, :] = jnp.broadcast_to(place_of.astype(F32), (1, LANES))
+        spaced_ref[i : i + 1, :] = jnp.full((1, LANES), float(order[i]), F32)
     ids_ref[...] = spaced_ref[:count, :].astype(BF16)
     write_nodes(nodes_ref)
     loads[0].wait()
     place(count, rank_ref, ids_ref, block_ref, lane_ref)
     loads[1].wait()
     loads[2].wait()
-    half = count // 2
-    for part in range(2):
+    for part in (0, 1):
         scatter(
             part * half, half, rank_ref, coords_ref, slot_ref, block_ref, lane_ref, ids_ref, send_ref, acc_ref
         )
         if part == 0:
             pl.semaphore_wait(barrier, count - 1)
-        for i in range(part * half, (part + 1) * half):
-            if i != own:
-                outward(i, peer(i)).start()
-    for b in range(BLOCKS):
-        recv_ref[b, own : own + 1, :] = send_ref[b, own : own + 1, :]
+        to_others(part * half, (part + 1) * half, functools.partial(send, send_ref, recv_ref, out_sem, in_sem))
+    keep(send_ref, recv_ref, in_sem)
     loads[3].wait()
     turn_fields(fields_ref, spaced_ref, turned_ref)
 
     def body(quad, _):
-        for j in range(32):
-
-            @pl.when(quad * 32 + j != own)
-            def _():
-                outward(quad * 32 + j, here).wait_recv()
-
+        wait_for(QUAD, recv_ref, in_sem.at[quad])
         for turn in range(5):
             spots = []
             for m in range(4):
-                row = pl.multiple_of(quad * 32 + 8 * (turn if turn < 4 else m), 8)
+                row = pl.multiple_of(quad * QUAD + 8 * (turn if turn < 4 else m), 8)
                 spots.append((m if turn < 4 else 4, pl.ds(row, 8)))
             rows = swap_groups([recv_ref[b, at, :] for b, at in spots])
             values = swap_groups(interpolate(rows, turned_ref, nodes_ref))
@@ -330,33 +319,28 @@
 
             @pl.when(quad == g)
             def _():
-                for i in range(32 * g, 32 * g + 32):
-                    if i != own:
-                        backward(i, peer(i)).start()
+                to_others(
+                    QUAD * g,
+                    QUAD * g + QUAD,
+                    functools.partial(send, values_ref, back_ref, back_out_sem, back_in_sem),
+                )
 
         return 0
 
     lax.fori_loop(0, quads, body, 0)
-    for b in range(BLOCKS):
-        back_ref[b, own : own + 1, :] = values_ref[b, own : own + 1, :]
-
-    def finish(i, _):
-        @pl.when(i != own)
-        def _():
-            outward(i, here).wait_send()
-            backward(i, here).wait()
-
-        return 0
-
-    early = count - 32
-    lax.fori_loop(0, early, finish, 0)
+    keep(values_ref, back_ref, back_in_sem)
+    early = count - QUAD
+    for quad in range(quads - 1):
+        wait_for(QUAD, back_ref, back_in_sem.at[quad])
     rows = [back_ref[b, :early, :] for b in range(BLOCKS)]
     rows.append(jnp.zeros((-BLOCKS * early % LANES, LANES), F32))
     table_ref[...] = jnp.concatenate(rows, axis=0).T.astype(BF16)
     pick(table_ref, ids_ref[:early, :], rank_ref, block_ref, lane_ref, None, part_ref)
-    lax.fori_loop(early, count, finish, 0)
+    wait_for(QUAD, back_ref, back_in_sem.at[quads - 1])
     for b in range(BLOCKS):
-        late_ref[b * 32 : (b + 1) * 32, :] = back_ref[b, early:, :]
+        late_ref[b * QUAD : (b + 1) * QUAD, :] = back_ref[b, early:, :]
+    wait_for(count - 1, send_ref, out_sem.at[0])
+    wait_for(count - 1, values_ref, back_out_sem.at[0])
 
 
 def pick(table_ref, ids, rank_ref, block_ref, lane_ref, part_ref, out_ref):
@@ -413,9 +397,8 @@
     line = jax.ShapeDtypeStruct((1, probes), F32)
 
     buffer = pltpu.VMEM((BLOCKS, count, LANES), F32)
-    arrivals = pltpu.SemaphoreType.DMA((count,))
     rank = element_rank.reshape(1, probes)
-    late = BLOCKS * 32
+    late = BLOCKS * QUAD
     whole = jax.ShapeDtypeStruct((4, probes), F32)
     part, returned, block, lane, ids = call(
         functools.partial(sample_kernel, sizes),
@@ -431,7 +414,7 @@
             pltpu.VMEM((BLOCKS * count // 2, 2 * LANES), F32),
             pltpu.VMEM((256 * 8, elements), F32),
             pltpu.VMEM((256, 8 * elements), BF16),
-            pltpu.VMEM((LANES, -(-BLOCKS * (count - 32) // LANES) * LANES), BF16),
+            pltpu.VMEM((LANES, -(-BLOCKS * (count - QUAD) // LANES) * LANES), BF16),
         ]
         + [
             pltpu.VMEM((64, LANES), F32),
@@ -441,8 +424,7 @@
             pltpu.VMEM(fields.shape, BF16),
         ]
         + [buffer] * 4
-        + [pltpu.SemaphoreType.DMA((4,))]
-        + [arrivals] * 4,
+        + [pltpu.SemaphoreType.DMA((n,)) for n in (4, 1, count // QUAD, 1, count // QUAD)],
         collective_id=0,
         has_side_effects=True,
     )(

time: 44.5 us -> 41.1 us (0.924)
  the two profiles are of different devices: /device:TPU:1 before, /device:TPU:63 now
where the time goes in v4:
time: 41.1 us; the launch traced here: 40.9 us
  Pallas kernels  40.9 us (100%)
    pallas_call x1, Pallas kernels, local(): call(functools.partial(sample_kernel, sizes), [HBM] * 4, (whole, jax.Shap...  38 us
    pallas_call x1, Pallas kernels, local(): call(return_kernel, [VMEM] * 6, whole, [pltpu.VMEM((LANES, -(-late // LAN...  2.94 us

profile of v4, /device:TPU:63, one launch (start us, length us, event | category | flops | bytes accessed | tf_op | source)
XLA Modules:
  0.0 40.9 jit_solution(8204281798091504450)
XLA Ops:
  0.0 0.0 copy-start
  0.0 38.0 %shard_map.46 = (f32[4,16384]{1,0:T(4,128)S(1)}, f32[160,128]{1,0:T(8,128)S(1)}, f32[1,16384]{1,0:T(1,128)S(1)}, f32[1,16384]{1,0:T(1,128)S(1)}, bf16[128,128]{1,0:T(8,128)(2,1)S(1)}) custom-call(s32[1,16384]{1,0:T(1,128)} %bitcast.2, f32[3,16384]{1,0:T(4,128)} %coords_hbm.1, s32[1,16384]{1,0:T(1,128)} %bitcast.4, bf16[128,2048]{1,0:T(8,128)(2,1)} %fields_hbm.1), custom_call_target="tpu_custom_call" | custom-call | tf_op jit(solution)/shard_map/pallas_call | solution.py:403
  38.0 0.0 copy-done
  38.0 2.9 %shard_map.47 = f32[4,16384]{1,0:T(4,128)} custom-call(f32[160,128]{1,0:T(8,128)S(1)} %get-tuple-element.10.late_ref, f32[4,16384]{1,0:T(4,128)S(1)} %get-tuple-element.11.part_ref, s32[1,16384]{1,0:T(1,128)S(1)} %bitcast.3, f32[1,16384]{1,0:T(1,128)S(1)} %get-tuple-element.12.block_ref, f32[1,16384]{1,0:T(1,128)S(1)} %get-tuple-element.13.lane_ref, ...), custom_call_target="tpu_custom_call" | custom-call | tf_op jit(solution)/shard_map/pallas_call | solution.py:436
Async XLA Ops:
  0.0 38.0 %copy-start = (s32[16384,1]{0,1:T(1,128)S(1)}, s32[16384,1]{0,1:T(1,128)}, u32[]{:S(2)}) copy-start(s32[16384,1]{0,1:T(1,128)} %param.6) | copy-start | bytes 196612

commit v5 on v4

--- a/solution.py
+++ b/solution.py
@@ -15,9 +15,9 @@
 PIECE = 32
 BLOCKS = 5
 QUAD = 32
-PLACED = 16
-GATHERED = 16
-RETURNED = 16
+PLACED = 32
+GATHERED = 32
+RETURNED = 32
 
 gll_points = np.array(
     [
@@ -93,9 +93,10 @@
     lax.fori_loop(0, probes // (CHUNK * PLACED), body, jnp.zeros((count, LANES), BF16))
 
 
-def scatter(first, many, rank_ref, coords_ref, slot_ref, block_ref, lane_ref, ids_ref, send_ref, acc_ref):
+def scatter(rank_ref, coords_ref, slot_ref, block_ref, lane_ref, ids_ref, send_ref, acc_ref):
     probes = rank_ref.shape[1]
-    ids = twice(ids_ref[first : first + many, :])
+    many = ids_ref.shape[0]
+    ids = twice(ids_ref[...])
     lane_ids = iota_bf16((PIECE, CHUNK))
     zero = jnp.zeros((), BF16)
     acc_ref[...] = jnp.zeros_like(acc_ref)
@@ -132,7 +133,7 @@
     lax.fori_loop(0, probes // (GATHERED * CHUNK), body, 0)
     for b in range(BLOCKS):
         rows = slice(b * many, (b + 1) * many)
-        send_ref[b, first : first + many, :] = acc_ref[rows, :LANES] + acc_ref[rows, LANES:]
+        send_ref[b] = acc_ref[rows, :LANES] + acc_ref[rows, LANES:]
 
 
 def swap_groups(rows):
@@ -217,6 +218,7 @@
     late_ref,
     block_ref,
     lane_ref,
+    late_ids_ref,
     ids_ref,
     acc_ref,
     spaced_ref,
@@ -292,18 +294,27 @@
     place(count, rank_ref, ids_ref, block_ref, lane_ref)
     loads[1].wait()
     loads[2].wait()
-    for part in (0, 1):
-        scatter(
-            part * half, half, rank_ref, coords_ref, slot_ref, block_ref, lane_ref, ids_ref, send_ref, acc_ref
-        )
-        if part == 0:
-            pl.semaphore_wait(barrier, count - 1)
-        to_others(part * half, (part + 1) * half, functools.partial(send, send_ref, recv_ref, out_sem, in_sem))
+    scatter(rank_ref, coords_ref, slot_ref, block_ref, lane_ref, ids_ref, send_ref, acc_ref)
+    pl.semaphore_wait(barrier, count - 1)
+
+    def ask(phase, _):
+        for h in range(2):
+
+            @pl.when((phase + own // QUAD) % 2 == h)
+            def _():
+                to_others(h * half, (h + 1) * half, functools.partial(send, send_ref, recv_ref, out_sem, in_sem))
+
+        return 0
+
+    lax.fori_loop(0, 2, ask, 0)
     keep(send_ref, recv_ref, in_sem)
     loads[3].wait()
     turn_fields(fields_ref, spaced_ref, turned_ref)
 
-    def body(quad, _):
+    side = own // half
+
+    def body(step, _):
+        quad = step + side * (1 - 2 * (step % 2))
         wait_for(QUAD, recv_ref, in_sem.at[quad])
         for turn in range(5):
             spots = []
@@ -329,18 +340,25 @@
 
     lax.fori_loop(0, quads, body, 0)
     keep(values_ref, back_ref, back_in_sem)
-    early = count - QUAD
-    for quad in range(quads - 1):
-        wait_for(QUAD, back_ref, back_in_sem.at[quad])
-    rows = [back_ref[b, :early, :] for b in range(BLOCKS)]
-    rows.append(jnp.zeros((-BLOCKS * early % LANES, LANES), F32))
-    table_ref[...] = jnp.concatenate(rows, axis=0).T.astype(BF16)
-    pick(table_ref, ids_ref[:early, :], rank_ref, block_ref, lane_ref, None, part_ref)
-    wait_for(QUAD, back_ref, back_in_sem.at[quads - 1])
-    for b in range(BLOCKS):
-        late_ref[b * QUAD : (b + 1) * QUAD, :] = back_ref[b, early:, :]
+    first = own // QUAD % 2
+    table_ref[...] = answers(first, half, back_ref, functools.partial(wait_for, QUAD), back_in_sem).T.astype(BF16)
+    pick(table_ref, ids_ref[halves(first, half), :], rank_ref, block_ref, lane_ref, None, part_ref)
+    late_ref[...] = answers(1 - first, half, back_ref, functools.partial(wait_for, QUAD), back_in_sem)
+    late_ids_ref[...] = ids_ref[halves(1 - first, half), :]
     wait_for(count - 1, send_ref, out_sem.at[0])
     wait_for(count - 1, values_ref, back_out_sem.at[0])
+
+
+def halves(which, half):
+    return pl.ds(pl.multiple_of(which * half, half), half)
+
+
+def answers(which, half, back_ref, wait, back_in_sem):
+    for k in range(half // QUAD):
+        wait(back_ref, back_in_sem.at[which * (half // QUAD) + k])
+    rows = [back_ref[b, halves(which, half), :] for b in range(BLOCKS)]
+    rows.append(jnp.zeros((-BLOCKS * half % LANES, LANES), F32))
+    return jnp.concatenate(rows, axis=0)
 
 
 def pick(table_ref, ids, rank_ref, block_ref, lane_ref, part_ref, out_ref):
@@ -369,10 +387,8 @@
 
 
 def return_kernel(late_ref, part_ref, rank_ref, block_ref, lane_ref, ids_ref, out_ref, table_ref):
-    late = late_ref.shape[0]
-    rows = jnp.concatenate([late_ref[...], jnp.zeros((-late % LANES, LANES), F32)], axis=0)
-    table_ref[...] = rows.T.astype(BF16)
-    pick(table_ref, ids_ref[-(late // BLOCKS) :, :], rank_ref, block_ref, lane_ref, part_ref, out_ref)
+    table_ref[...] = late_ref[...].T.astype(BF16)
+    pick(table_ref, ids_ref[...], rank_ref, block_ref, lane_ref, part_ref, out_ref)
 
 
 VMEM = pl.BlockSpec(memory_space=pltpu.VMEM)
@@ -398,7 +414,7 @@
 
     buffer = pltpu.VMEM((BLOCKS, count, LANES), F32)
     rank = element_rank.reshape(1, probes)
-    late = BLOCKS * QUAD
+    late = -(-BLOCKS * (count // 2) // LANES) * LANES
     whole = jax.ShapeDtypeStruct((4, probes), F32)
     part, returned, block, lane, ids = call(
         functools.partial(sample_kernel, sizes),
@@ -408,13 +424,14 @@
             jax.ShapeDtypeStruct((late, LANES), F32),
             line,
             line,
-            jax.ShapeDtypeStruct((count, LANES), BF16),
+            jax.ShapeDtypeStruct((count // 2, LANES), BF16),
         ),
         [
-            pltpu.VMEM((BLOCKS * count // 2, 2 * LANES), F32),
+            pltpu.VMEM((count, LANES), BF16),
+            pltpu.VMEM((BLOCKS * count, 2 * LANES), F32),
             pltpu.VMEM((256 * 8, elements), F32),
             pltpu.VMEM((256, 8 * elements), BF16),
-            pltpu.VMEM((LANES, -(-BLOCKS * (count - QUAD) // LANES) * LANES), BF16),
+            pltpu.VMEM((LANES, late), BF16),
         ]
         + [
             pltpu.VMEM((64, LANES), F32),
@@ -437,7 +454,7 @@
         return_kernel,
         [VMEM] * 6,
         whole,
-        [pltpu.VMEM((LANES, -(-late // LANES) * LANES), BF16)],
+        [pltpu.VMEM((LANES, late), BF16)],
     )(returned, part, rank, block, lane, ids)
 
 

time: 41.1 us -> 38.4 us (0.934)
  the two profiles are of different devices: /device:TPU:63 before, /device:TPU:47 now
where the time goes in v5:
time: 38.4 us; the launch traced here: 38.3 us
  Pallas kernels  38.3 us (100%)
    pallas_call x1, Pallas kernels, local(): call(functools.partial(sample_kernel, sizes), [HBM] * 4, (whole, jax.Shap...  34.9 us
    pallas_call x1, Pallas kernels, local(): call(return_kernel, [VMEM] * 6, whole, [pltpu.VMEM((LANES, late), BF16)])  3.4 us

profile of v5, /device:TPU:47, one launch (start us, length us, event | category | flops | bytes accessed | tf_op | source)
XLA Modules:
  0.0 38.3 jit_solution(17406159672004968153)
XLA Ops:
  0.0 0.0 copy-start
  0.0 34.9 %shard_map.46 = (f32[4,16384]{1,0:T(4,128)S(1)}, f32[384,128]{1,0:T(8,128)S(1)}, f32[1,16384]{1,0:T(1,128)S(1)}, f32[1,16384]{1,0:T(1,128)S(1)}, bf16[64,128]{1,0:T(8,128)(2,1)S(1)}) custom-call(s32[1,16384]{1,0:T(1,128)} %bitcast.2, f32[3,16384]{1,0:T(4,128)} %coords_hbm.1, s32[1,16384]{1,0:T(1,128)} %bitcast.4, bf16[128,2048]{1,0:T(8,128)(2,1)} %fields_hbm.1), custom_call_target="tpu_custom_call" | custom-call | tf_op jit(solution)/shard_map/pallas_call | solution.py:419
  34.9 0.0 copy-done
  34.9 3.4 %shard_map.47 = f32[4,16384]{1,0:T(4,128)} custom-call(f32[384,128]{1,0:T(8,128)S(1)} %get-tuple-element.10.late_ref, f32[4,16384]{1,0:T(4,128)S(1)} %get-tuple-element.11.part_ref, s32[1,16384]{1,0:T(1,128)S(1)} %bitcast.3, f32[1,16384]{1,0:T(1,128)S(1)} %get-tuple-element.12.block_ref, f32[1,16384]{1,0:T(1,128)S(1)} %get-tuple-element.13.lane_ref, ...), custom_call_target="tpu_custom_call" | custom-call | tf_op jit(solution)/shard_map/pallas_call | solution.py:453
Async XLA Ops:
  0.0 34.9 %copy-start = (s32[16384,1]{0,1:T(1,128)S(1)}, s32[16384,1]{0,1:T(1,128)}, u32[]{:S(2)}) copy-start(s32[16384,1]{0,1:T(1,128)} %param.6) | copy-start | bytes 196612

commit v6 on v5

--- a/solution.py
+++ b/solution.py
@@ -218,7 +218,6 @@
     late_ref,
     block_ref,
     lane_ref,
-    late_ids_ref,
     ids_ref,
     acc_ref,
     spaced_ref,
@@ -311,7 +310,7 @@
     loads[3].wait()
     turn_fields(fields_ref, spaced_ref, turned_ref)
 
-    side = own // half
+    side = own // (count - QUAD)
 
     def body(step, _):
         quad = step + side * (1 - 2 * (step % 2))
@@ -340,55 +339,89 @@
 
     lax.fori_loop(0, quads, body, 0)
     keep(values_ref, back_ref, back_in_sem)
-    first = own // QUAD % 2
-    table_ref[...] = answers(first, half, back_ref, functools.partial(wait_for, QUAD), back_in_sem).T.astype(BF16)
-    pick(table_ref, ids_ref[halves(first, half), :], rank_ref, block_ref, lane_ref, None, part_ref)
-    late_ref[...] = answers(1 - first, half, back_ref, functools.partial(wait_for, QUAD), back_in_sem)
-    late_ids_ref[...] = ids_ref[halves(1 - first, half), :]
+    odd = own // QUAD % 2
+    split = count - QUAD
+    for flag, early, late in ((0, (0, split), (split, count)), (1, (split, count), (0, split))):
+
+        @pl.when(odd == flag)
+        def _():
+            table = answers(early, back_ref, functools.partial(wait_for, QUAD), back_in_sem)
+            table_ref[:, : table.shape[0]] = table.T.astype(BF16)
+            pick(
+                table_ref.at[:, : table.shape[0]], ids_ref[slice(*early), :], rank_ref, block_ref, lane_ref, None, part_ref
+            )
+            table = answers(late, back_ref, functools.partial(wait_for, QUAD), back_in_sem)
+            late_ref[: table.shape[0], :] = table
+
     wait_for(count - 1, send_ref, out_sem.at[0])
     wait_for(count - 1, values_ref, back_out_sem.at[0])
 
 
-def halves(which, half):
-    return pl.ds(pl.multiple_of(which * half, half), half)
-
-
-def answers(which, half, back_ref, wait, back_in_sem):
-    for k in range(half // QUAD):
-        wait(back_ref, back_in_sem.at[which * (half // QUAD) + k])
-    rows = [back_ref[b, halves(which, half), :] for b in range(BLOCKS)]
-    rows.append(jnp.zeros((-BLOCKS * half % LANES, LANES), F32))
+def padded(many):
+    return -(-BLOCKS * many // LANES) * LANES
+
+
+def answers(span, back_ref, wait, back_in_sem):
+    first, last = span
+    for k in range(first // QUAD, last // QUAD):
+        wait(back_ref, back_in_sem.at[k])
+    rows = [back_ref[b, first:last, :] for b in range(BLOCKS)]
+    rows.append(jnp.zeros((padded(last - first) - BLOCKS * (last - first), LANES), F32))
     return jnp.concatenate(rows, axis=0)
 
 
 def pick(table_ref, ids, rank_ref, block_ref, lane_ref, part_ref, out_ref):
     probes = rank_ref.shape[1]
     ids = twice(ids)
+    raised = ids + float(LANES)
     lane_ids = lax.broadcasted_iota(jnp.int32, (PIECE, CHUNK), 0).astype(F32)
+    row_ids = lax.broadcasted_iota(jnp.int32, (8, CHUNK), 0)
+
+    def merge(a, b, shift):
+        lower = (row_ids // shift) % 2 == 0
+        return jnp.where(lower, a, b) + pltpu.roll(jnp.where(lower, b, a), shift, 0)
 
     def body(step, _):
         for g in range(RETURNED):
             at = chunk_at(step, g, RETURNED)
             rank, block = rank_ref[:, at].astype(F32), block_ref[:, at]
-            hots = [one_hot(ids, jnp.where(block == float(b), rank, -1.0)) for b in range(BLOCKS)]
+            code = rank + block * float(LANES)
+            hots = []
+            for b in range(0, BLOCKS, 2):
+                inside = (block >= float(b)) & (block < float(b + 2))
+                row = jnp.where(inside, code - float(b * LANES), -1.0)
+                hots += [one_hot(known, row) for known in (ids, raised)[: BLOCKS - b]]
             spare = table_ref.shape[1] - BLOCKS * ids.shape[0]
             if spare:
                 hots.append(jnp.zeros((spare, CHUNK), BF16))
             picked = jnp.dot(table_ref[...], jnp.concatenate(hots, axis=0), preferred_element_type=F32)
             here = lane_ids == jnp.broadcast_to(lane_ref[:, at], (PIECE, CHUNK))
+            sums = []
             for f in range(4):
-                value = jnp.sum(
-                    jnp.where(here, picked[f * PIECE : (f + 1) * PIECE], 0.0), axis=0, keepdims=True
-                )
-                out_ref[f : f + 1, at] = value if part_ref is None else value + part_ref[f : f + 1, at]
+                chosen = jnp.where(here, picked[f * PIECE : (f + 1) * PIECE], 0.0)
+                sums.append(sum(chosen[8 * k : 8 * k + 8] for k in range(PIECE // 8)))
+            mixed = merge(merge(sums[0], sums[1], 1), merge(sums[2], sums[3], 1), 2)
+            value = (mixed + pltpu.roll(mixed, 4, 0))[:4]
+            out_ref[:, at] = value if part_ref is None else value + part_ref[:, at]
         return 0
 
     lax.fori_loop(0, probes // (RETURNED * CHUNK), body, 0)
 
 
-def return_kernel(late_ref, part_ref, rank_ref, block_ref, lane_ref, ids_ref, out_ref, table_ref):
-    table_ref[...] = late_ref[...].T.astype(BF16)
-    pick(table_ref, ids_ref[...], rank_ref, block_ref, lane_ref, part_ref, out_ref)
+def return_kernel(sizes, late_ref, part_ref, rank_ref, block_ref, lane_ref, ids_ref, out_ref, table_ref):
+    count = ids_ref.shape[0]
+    own = (lax.axis_index("gx") * sizes[1] + lax.axis_index("gy")) * sizes[2] + lax.axis_index("gz")
+    odd = jnp.int32(0)
+    for i, rank in enumerate(served(sizes)):
+        odd = jnp.where(own == rank, i // QUAD % 2, odd)
+    split = count - QUAD
+    for flag, (first, last) in enumerate(((split, count), (0, split))):
+
+        @pl.when(odd == flag)
+        def _():
+            rows = padded(last - first)
+            table_ref[:, :rows] = late_ref[:rows, :].T.astype(BF16)
+            pick(table_ref.at[:, :rows], ids_ref[first:last, :], rank_ref, block_ref, lane_ref, part_ref, out_ref)
 
 
 VMEM = pl.BlockSpec(memory_space=pltpu.VMEM)
@@ -414,7 +447,7 @@
 
     buffer = pltpu.VMEM((BLOCKS, count, LANES), F32)
     rank = element_rank.reshape(1, probes)
-    late = -(-BLOCKS * (count // 2) // LANES) * LANES
+    late = padded(count - QUAD)
     whole = jax.ShapeDtypeStruct((4, probes), F32)
     part, returned, block, lane, ids = call(
         functools.partial(sample_kernel, sizes),
@@ -424,10 +457,9 @@
             jax.ShapeDtypeStruct((late, LANES), F32),
             line,
             line,
-            jax.ShapeDtypeStruct((count // 2, LANES), BF16),
+            jax.ShapeDtypeStruct((count, LANES), BF16),
         ),
         [
-            pltpu.VMEM((count, LANES), BF16),
             pltpu.VMEM((BLOCKS * count, 2 * LANES), F32),
             pltpu.VMEM((256 * 8, elements), F32),
             pltpu.VMEM((256, 8 * elements), BF16),
@@ -451,7 +483,7 @@
         ]
     )
     return call(
-        return_kernel,
+        functools.partial(return_kernel, sizes),
         [VMEM] * 6,
         whole,
         [pltpu.VMEM((LANES, late), BF16)],

time: 38.4 us -> 37.7 us (0.982)
  Pallas kernels: 38.3 us -> 37.5 us
    pallas_call x1, Pallas kernels: 3.4 us -> 2.68 us  [local(): call(functools.partial(return_kernel, sizes), [VMEM] * 6, whole, [pltpu.V...]
where the time goes in v6:
time: 37.7 us; the launch traced here: 37.5 us
  Pallas kernels  37.5 us (99%)
    pallas_call x1, Pallas kernels, local(): call(functools.partial(sample_kernel, sizes), [HBM] * 4, (whole, jax.Shap...  34.8 us
    pallas_call x1, Pallas kernels, local(): call(functools.partial(return_kernel, sizes), [VMEM] * 6, whole, [pltpu.V...  2.68 us

profile of v6, /device:TPU:47, one launch (start us, length us, event | category | flops | bytes accessed | tf_op | source)
XLA Modules:
  0.0 37.5 jit_solution(18383749206478318674)
XLA Ops:
  0.0 0.0 copy-start
  0.0 34.8 %shard_map.46 = (f32[4,16384]{1,0:T(4,128)S(1)}, f32[512,128]{1,0:T(8,128)S(1)}, f32[1,16384]{1,0:T(1,128)S(1)}, f32[1,16384]{1,0:T(1,128)S(1)}, bf16[128,128]{1,0:T(8,128)(2,1)S(1)}) custom-call(s32[1,16384]{1,0:T(1,128)} %bitcast.2, f32[3,16384]{1,0:T(4,128)} %coords_hbm.1, s32[1,16384]{1,0:T(1,128)} %bitcast.4, bf16[128,2048]{1,0:T(8,128)(2,1)} %fields_hbm.1), custom_call_target="tpu_custom_call" | custom-call | tf_op jit(solution)/shard_map/pallas_call | solution.py:452
  34.9 0.0 copy-done
  34.9 2.7 %shard_map.47 = f32[4,16384]{1,0:T(4,128)} custom-call(f32[512,128]{1,0:T(8,128)S(1)} %get-tuple-element.10.late_ref, f32[4,16384]{1,0:T(4,128)S(1)} %get-tuple-element.11.part_ref, s32[1,16384]{1,0:T(1,128)S(1)} %bitcast.3, f32[1,16384]{1,0:T(1,128)S(1)} %get-tuple-element.12.block_ref, f32[1,16384]{1,0:T(1,128)S(1)} %get-tuple-element.13.lane_ref, ...), custom_call_target="tpu_custom_call" | custom-call | tf_op jit(solution)/shard_map/pallas_call | solution.py:485
Async XLA Ops:
  0.0 34.9 %copy-start = (s32[16384,1]{0,1:T(1,128)S(1)}, s32[16384,1]{0,1:T(1,128)}, u32[]{:S(2)}) copy-start(s32[16384,1]{0,1:T(1,128)} %param.6) | copy-start | bytes 196612

commit v7 on v6

--- a/solution.py
+++ b/solution.py
@@ -313,7 +313,7 @@
     side = own // (count - QUAD)
 
     def body(step, _):
-        quad = step + side * (1 - 2 * (step % 2))
+        quad = step + side * (step // 2) * (1 - 2 * (step % 2))
         wait_for(QUAD, recv_ref, in_sem.at[quad])
         for turn in range(5):
             spots = []

time: 37.7 us -> 37.5 us (level)
  the two profiles are of different devices: /device:TPU:47 before, /device:TPU:63 now
where the time goes in v7:
time: 37.5 us; the launch traced here: 37.3 us
  Pallas kernels  37.3 us (99%)
    pallas_call x1, Pallas kernels, local(): call(functools.partial(sample_kernel, sizes), [HBM] * 4, (whole, jax.Shap...  33.8 us
    pallas_call x1, Pallas kernels, local(): call(functools.partial(return_kernel, sizes), [VMEM] * 6, whole, [pltpu.V...  3.48 us

profile of v7, /device:TPU:63, one launch (start us, length us, event | category | flops | bytes accessed | tf_op | source)
XLA Modules:
  0.0 37.3 jit_solution(7191626313058938799)
XLA Ops:
  0.0 0.0 copy-start
  0.0 33.8 %shard_map.46 = (f32[4,16384]{1,0:T(4,128)S(1)}, f32[512,128]{1,0:T(8,128)S(1)}, f32[1,16384]{1,0:T(1,128)S(1)}, f32[1,16384]{1,0:T(1,128)S(1)}, bf16[128,128]{1,0:T(8,128)(2,1)S(1)}) custom-call(s32[1,16384]{1,0:T(1,128)} %bitcast.2, f32[3,16384]{1,0:T(4,128)} %coords_hbm.1, s32[1,16384]{1,0:T(1,128)} %bitcast.4, bf16[128,2048]{1,0:T(8,128)(2,1)} %fields_hbm.1), custom_call_target="tpu_custom_call" | custom-call | tf_op jit(solution)/shard_map/pallas_call | solution.py:452
  33.9 0.0 copy-done
  33.9 3.5 %shard_map.47 = f32[4,16384]{1,0:T(4,128)} custom-call(f32[512,128]{1,0:T(8,128)S(1)} %get-tuple-element.10.late_ref, f32[4,16384]{1,0:T(4,128)S(1)} %get-tuple-element.11.part_ref, s32[1,16384]{1,0:T(1,128)S(1)} %bitcast.3, f32[1,16384]{1,0:T(1,128)S(1)} %get-tuple-element.12.block_ref, f32[1,16384]{1,0:T(1,128)S(1)} %get-tuple-element.13.lane_ref, ...), custom_call_target="tpu_custom_call" | custom-call | tf_op jit(solution)/shard_map/pallas_call | solution.py:485
Async XLA Ops:
  0.0 33.9 %copy-start = (s32[16384,1]{0,1:T(1,128)S(1)}, s32[16384,1]{0,1:T(1,128)}, u32[]{:S(2)}) copy-start(s32[16384,1]{0,1:T(1,128)} %param.6) | copy-start | bytes 196612

commit v8 on v7

--- a/solution.py
+++ b/solution.py
@@ -299,7 +299,7 @@
     def ask(phase, _):
         for h in range(2):
 
-            @pl.when((phase + own // QUAD) % 2 == h)
+            @pl.when((phase + (own // QUAD + 1) // 2 + 1) % 2 == h)
             def _():
                 to_others(h * half, (h + 1) * half, functools.partial(send, send_ref, recv_ref, out_sem, in_sem))
 

time: 37.5 us -> 38.1 us (1.016)
  the two profiles are of different devices: /device:TPU:63 before, /device:TPU:1 now
where the time goes in v8:
time: 38.1 us; the launch traced here: 37.5 us
  Pallas kernels  37.5 us (98%)
    pallas_call x1, Pallas kernels, local(): call(functools.partial(sample_kernel, sizes), [HBM] * 4, (whole, jax.Shap...  34.8 us
    pallas_call x1, Pallas kernels, local(): call(functools.partial(return_kernel, sizes), [VMEM] * 6, whole, [pltpu.V...  2.68 us

profile of v8, /device:TPU:1, one launch (start us, length us, event | category | flops | bytes accessed | tf_op | source)
XLA Modules:
  0.0 37.5 jit_solution(14841307702481181105)
XLA Ops:
  0.0 0.0 copy-start
  0.0 34.8 %shard_map.46 = (f32[4,16384]{1,0:T(4,128)S(1)}, f32[512,128]{1,0:T(8,128)S(1)}, f32[1,16384]{1,0:T(1,128)S(1)}, f32[1,16384]{1,0:T(1,128)S(1)}, bf16[128,128]{1,0:T(8,128)(2,1)S(1)}) custom-call(s32[1,16384]{1,0:T(1,128)} %bitcast.2, f32[3,16384]{1,0:T(4,128)} %coords_hbm.1, s32[1,16384]{1,0:T(1,128)} %bitcast.4, bf16[128,2048]{1,0:T(8,128)(2,1)} %fields_hbm.1), custom_call_target="tpu_custom_call" | custom-call | tf_op jit(solution)/shard_map/pallas_call | solution.py:452
  34.9 0.0 copy-done
  34.9 2.7 %shard_map.47 = f32[4,16384]{1,0:T(4,128)} custom-call(f32[512,128]{1,0:T(8,128)S(1)} %get-tuple-element.10.late_ref, f32[4,16384]{1,0:T(4,128)S(1)} %get-tuple-element.11.part_ref, s32[1,16384]{1,0:T(1,128)S(1)} %bitcast.3, f32[1,16384]{1,0:T(1,128)S(1)} %get-tuple-element.12.block_ref, f32[1,16384]{1,0:T(1,128)S(1)} %get-tuple-element.13.lane_ref, ...), custom_call_target="tpu_custom_call" | custom-call | tf_op jit(solution)/shard_map/pallas_call | solution.py:485
Async XLA Ops:
  0.0 34.9 %copy-start = (s32[16384,1]{0,1:T(1,128)S(1)}, s32[16384,1]{0,1:T(1,128)}, u32[]{:S(2)}) copy-start(s32[16384,1]{0,1:T(1,128)} %param.6) | copy-start | bytes 196612
